TPU v7x, 512 devices: a whole 4x8x8 slice. The times are simulated.
512 devices in a mesh: head: 8 (over y_hi, core), blk: 64 (over z, y_lo, x).
Axes of the slice: x: 4, y: 8 (y_hi: 4, y_lo: 2; y = y_hi * 2 + y_lo), z: 8, core: 2. Of those that a mesh axis runs over, the one named last changes fastest.
Arguments:
- query_rows: bfloat16 [64, 144, 3072], P('blk', 'head'), may hold values from -6 to 6
- key_rows: bfloat16 [64, 144, 3072], P('blk', 'head'), may hold values from -6 to 6
- value_rows: bfloat16 [64, 144, 3072], P('blk', 'head'), may hold values from -6 to 6
- query_tangent: bfloat16 [64, 144, 3072], P('blk', 'head'), may hold values from -6 to 6
- key_tangent: bfloat16 [64, 144, 3072], P('blk', 'head'), may hold values from -6 to 6
- value_tangent: bfloat16 [64, 144, 3072], P('blk', 'head'), may hold values from -6 to 6
- query_gain: float32 [128], replicated, may hold values from 1 to 6
- key_gain: float32 [128], replicated, may hold values from 1 to 6
Outputs:
- attended: bfloat16 [64, 144, 3072], P('blk', 'head')
- attended_tangent: bfloat16 [64, 144, 3072], P('blk', 'head')
All inputs are finite; a program needn't handle non-finite values.
Results may differ from a plain program's by a relative error of at most 0.014.
The roundings to bfloat16 on the way count: a program that leaves them out, or rounds other values in their place, can miss the bound.
Values may be sent and summed in bfloat16 or wider, within the bound.
A program may use at most 64 MiB of HBM per device.

v0:
```python
import math

import jax
import jax.numpy as jnp
from jax import lax
from jax.sharding import PartitionSpec as P

HD = 128
TXT = 512
GRID_W = 64
GROUP = 16


EPSILON = 1e-06
THETA = 10000.0


def in_one_piece(arrays, axis, split_dim, concat_dim, along):
    both = jnp.concatenate(arrays, axis=along)
    out, at, finished = (
        lax.all_to_all(both, axis, split_axis=split_dim, concat_axis=concat_dim, tiled=True),
        0,
        [],
    )
    for a in arrays:
        finished.append(lax.slice_in_dim(out, at, at + a.shape[along], axis=along))
        at += a.shape[along]
    return tuple(finished)


def passed_along(block, axis, distance):
    devices = range(lax.axis_size(axis))
    route = [((i - distance) % len(devices), i) for i in devices]
    return lax.ppermute(block, axis, route)


def rotation(first, count, head_dim):
    block_offsets = first + jnp.arange(count, dtype=jnp.int32)
    is_image = block_offsets >= TXT
    patch = jnp.maximum(block_offsets - TXT, 0)
    row_id = jnp.where(is_image, patch // GRID_W, 0).astype(jnp.float32)
    column_id = jnp.where(is_image, patch % GRID_W, 0).astype(jnp.float32)
    leading = head_dim // 8
    lateral = (head_dim - leading) // 2
    exponent = jnp.arange(lateral // 2, dtype=jnp.float32) * (2.0 / lateral)
    frequency = jnp.exp(-math.log(THETA) * exponent)
    angles = jnp.concatenate(
        [
            jnp.zeros((count, leading // 2), jnp.float32),
            row_id[:, None] * frequency[None, :],
            column_id[:, None] * frequency[None, :],
        ],
        axis=1,
    )
    angles = jnp.repeat(angles, 2, axis=1)
    return (jnp.cos(angles), jnp.sin(angles))


def rotation_partner(head_dim):
    across = jnp.arange(head_dim, dtype=jnp.int32)
    lower = across[:, None]
    upper = across[None, :]
    forward = ((upper == lower + 1) & (lower % 2 == 0)).astype(jnp.float32)
    backward = ((lower == upper + 1) & (upper % 2 == 0)).astype(jnp.float32)
    return forward - backward


def normalize(raw, tangent, gain, cosine, sine, partner):
    values = raw.astype(jnp.float32)
    motion = tangent.astype(jnp.float32)
    inverse = lax.rsqrt(jnp.mean(values * values, axis=-1, keepdims=True) + EPSILON)
    coupling = jnp.mean(values * motion, axis=-1, keepdims=True)
    normed = values * inverse * gain
    normalized_tangent = gain * (motion * inverse - values * inverse * inverse * inverse * coupling)

    def rotate(feature_field):
        return (
            feature_field * cosine
            + jnp.dot(feature_field, partner, precision=lax.Precision.HIGHEST) * sine
        )

    return (rotate(normed).astype(jnp.bfloat16), rotate(normalized_tangent).astype(jnp.bfloat16))


def local(
    query_rows,
    key_rows,
    value_rows,
    query_tangent,
    key_tangent,
    value_tangent,
    query_gain,
    key_gain,
):
    arrived = in_one_piece(
        (query_rows, key_rows, value_rows, query_tangent, key_tangent, value_tangent),
        "head",
        2,
        1,
        0,
    )
    rows_here = arrived[0].shape[1]
    local_width = arrived[0].shape[2]
    heads_here = local_width // HD
    images = lax.axis_size("blk") // GROUP
    place = lax.axis_index("blk") // images

    def split_heads(feature_field):
        return feature_field[0].reshape(rows_here, heads_here, HD)

    cosine, sine = rotation(place * rows_here, rows_here, HD)
    cosine = cosine[:, None, :]
    sine = sine[:, None, :]
    partner = rotation_partner(HD)
    query_hat, query_dot = normalize(
        split_heads(arrived[0]), split_heads(arrived[3]), query_gain, cosine, sine, partner
    )
    key_hat, key_dot = normalize(
        split_heads(arrived[1]), split_heads(arrived[4]), key_gain, cosine, sine, partner
    )
    own_block = jnp.stack(
        [
            key_hat.reshape(rows_here, local_width),
            arrived[2][0],
            key_dot.reshape(rows_here, local_width),
            arrived[5][0],
        ],
        axis=0,
    )
    scale = 1.0 / math.sqrt(HD)
    query_pair = jnp.concatenate([query_dot, query_hat], axis=2)

    def absorb_segment(state, key_block):
        peak, total, drift, summed, summed_dot = state
        count = key_block.shape[1]
        block_key = key_block[0].reshape(count, heads_here, HD)
        block_value = key_block[1].reshape(count, heads_here, HD)
        block_key_dot = key_block[2].reshape(count, heads_here, HD)
        block_value_dot = key_block[3].reshape(count, heads_here, HD)
        logit_scores = (
            jnp.einsum("qhd,khd->hqk", query_hat, block_key, preferred_element_type=jnp.float32)
            * scale
        )
        key_pair = jnp.concatenate([block_key, block_key_dot], axis=2)
        score_dot = (
            jnp.einsum("qhd,khd->hqk", query_pair, key_pair, preferred_element_type=jnp.float32)
            * scale
        )
        new_peak = jnp.maximum(peak, jnp.max(logit_scores, axis=2, keepdims=True))
        rescale = jnp.exp(peak - new_peak)
        weights = jnp.exp(logit_scores - new_peak)
        product = weights * score_dot
        total = total * rescale + jnp.sum(weights, axis=2, keepdims=True)
        drift = drift * rescale + jnp.sum(product, axis=2, keepdims=True)
        low_weights = weights.astype(jnp.bfloat16)
        low_product = product.astype(jnp.bfloat16)
        summed = summed * rescale + jnp.einsum(
            "hqk,khd->hqd", low_weights, block_value, preferred_element_type=jnp.float32
        )
        summed_dot = (
            summed_dot * rescale
            + jnp.einsum(
                "hqk,khd->hqd", low_weights, block_value_dot, preferred_element_type=jnp.float32
            )
            + jnp.einsum(
                "hqk,khd->hqd", low_product, block_value, preferred_element_type=jnp.float32
            )
        )
        return (new_peak, total, drift, summed, summed_dot)

    def absorb(state, key_block):
        count = key_block.shape[1]
        span = 2 * rows_here
        return absorb_segment(state, key_block)

    state = (
        jnp.full((heads_here, rows_here, 1), -jnp.inf, jnp.float32),
        jnp.zeros((heads_here, rows_here, 1), jnp.float32),
        jnp.zeros((heads_here, rows_here, 1), jnp.float32),
        jnp.zeros((heads_here, rows_here, HD), jnp.float32),
        jnp.zeros((heads_here, rows_here, HD), jnp.float32),
    )

    def step_up(key_block):
        return passed_along(key_block, "blk", images)

    def both_step(counter, carry):
        carried, upward, downward = carry
        upward = step_up(upward)
        downward = passed_along(downward, "blk", -images)
        carried = absorb(carried, jnp.concatenate([upward, downward], axis=1))
        return (carried, upward, downward)

    state, upward, downward = lax.fori_loop(
        0, GROUP // 2 - 1, both_step, (state, own_block, own_block)
    )
    farthest = step_up(upward)
    state = absorb(state, jnp.concatenate([own_block, farthest], axis=1))
    peak, total, drift, summed, summed_dot = state
    attention_output = summed / total
    output_tangent = (summed_dot - drift / total * summed) / total
    attention_output = (
        attention_output.transpose(1, 0, 2)
        .reshape(rows_here, local_width)
        .astype(jnp.bfloat16)[None]
    )
    output_tangent = (
        output_tangent.transpose(1, 0, 2).reshape(rows_here, local_width).astype(jnp.bfloat16)[None]
    )
    returned = in_one_piece((attention_output, output_tangent), "head", 1, 2, 0)
    return (returned[0], returned[1])


def solution(mesh):
    in_specs = (
        P("blk", "head", None),
        P("blk", "head", None),
        P("blk", "head", None),
        P("blk", "head", None),
        P("blk", "head", None),
        P("blk", "head", None),
        P(),
        P(),
    )
    out_specs = (P("blk", "head", None), P("blk", "head", None))
    return jax.shard_map(local, mesh=mesh, in_specs=in_specs, out_specs=out_specs, check_vma=False)
```

profile of v0, /device:TPU:1, one launch (start us, length us, event | category | flops | bytes accessed | tf_op | source)
XLA Modules:
  0.0 283.4 jit_solution(160029324533516999)
XLA Ops:
  6.2 5.8 %copy.134 = bf16[6,18,3072]{1,0,2:T(8,128)(2,1)} copy(bf16[6,18,3072]{2,1,0:T(8,128)(2,1)S(1)} %constant_dynamic-update-slice_fusion.2) | data formatting | bytes 1327104 | tf_op jit(solution)/shard_map/concatenate | solution.py:19
  12.0 9.6 %reshape.168 = bf16[8,2,20736]{2,1,0:T(2,128)(2,1)} reshape(bf16[3072,6,18]{2,1,0:T(8,128)(2,1)} %bitcast.97) | data formatting | bytes 1327104
  21.5 10.3 %all-to-all-start = ((bf16[8,2,20736]{2,1,0:T(2,128)(2,1)}), bf16[8,2,20736]{2,1,0:T(2,128)(2,1)S(1)}, u32[]{:S(2)}, u32[]{:S(2)}) async-start(bf16[8,2,20736]{2,1,0:T(2,128)(2,1)} %reshape.168), calls=%async_computation | async-start | bytes 1327104 | tf_op jit(solution)/shard_map/all_to_all | solution.py:21
  32.8 17.2 %all-to-all-done = bf16[8,2,20736]{2,1,0:T(2,128)(2,1)S(1)} async-done(((bf16[8,2,20736]{2,1,0:T(2,128)(2,1)}), bf16[8,2,20736]{2,1,0:T(2,128)(2,1)S(1)}, u32[]{:S(2)}, u32[]{:S(2)}) %all-to-all-start) | async-done | bytes 663584 | tf_op jit(solution)/shard_map/all_to_all | solution.py:21
  50.0 8.0 %reshape.169 = bf16[3072,6,18]{2,1,0:T(8,128)(2,1)} reshape(bf16[8,2,20736]{2,1,0:T(2,128)(2,1)S(1)} %all-to-all-done) | data formatting | bytes 1327104
  58.1 6.4 %copy.135 = bf16[6,18,8,384]{3,1,2,0:T(8,128)(2,1)S(1)} copy(bf16[6,18,8,384]{1,0,3,2:T(8,128)(2,1)} %bitcast.98) | data formatting | bytes 1327104 | tf_op jit(solution)/shard_map/all_to_all | solution.py:21
  69.4 161.2 %while.23 = (s32[]{:T(128)}, f32[3,144,1]{1,0,2:T(4,128)S(1)}, f32[3,144,1]{1,0,2:T(4,128)S(1)}, f32[3,144,1]{1,0,2:T(4,128)S(1)}, f32[3,144,128]{2,1,0:T(8,128)...) while((s32[]{:T(128)}, f32[3,144,1]{1,0,2:T(4,128)S(1)}, ...), condition=%wide.region_8.9_spmd.clone, body=%wide.region_4.8_spmd.clone.sunk | while | flops 193995648 | bytes 17513496 | solution.py:194
  71.3 8.8 %collective-permute-start.1 = (bf16[4,144,384]{2,1,0:T(8,128)(2,1)S(1)}, bf16[4,144,384]{2,1,0:T(8,128)(2,1)S(1)}, u32[]{:S(2)}, u32[]{:S(2)}) collective-permute-start(bf16[4,144,384]{2,1,0:T(8,128)(2,1)S(1)} %get-tuple-element.271), channel_id=1, source_target_pairs={{4,0},{5,1},{6,2},{7,3},{8,4},{9,5},{10,6},{11,7},{12,8},{13,9},{1... | collective-permute-start | bytes 1327112 | tf_op jit(solution)/shard_map/while/body/eval_jaxpr/ppermute | solution.py:34
  80.0 7.7 %collective-permute-done = bf16[4,144,384]{2,1,0:T(8,128)(2,1)S(1)} collective-permute-done((bf16[4,144,384]{2,1,0:T(8,128)(2,1)S(1)}, bf16[4,144,384]{2,1,0:T(8,128)(2,1)S(1)}, u32[]{:S(2)}, u32[]{:S(2)}) %collective-permute-start) | collective-permute-done | bytes 442400 | tf_op jit(solution)/shard_map/while/body/eval_jaxpr/ppermute | solution.py:34
  96.2 7.9 %collective-permute-start.1 = (bf16[4,144,384]{2,1,0:T(8,128)(2,1)S(1)}, bf16[4,144,384]{2,1,0:T(8,128)(2,1)S(1)}, u32[]{:S(2)}, u32[]{:S(2)}) collective-permute-start(bf16[4,144,384]{2,1,0:T(8,128)(2,1)S(1)} %get-tuple-element.271), channel_id=1, source_target_pairs={{4,0},{5,1},{6,2},{7,3},{8,4},{9,5},{10,6},{11,7},{12,8},{13,9},{1... | collective-permute-start | bytes 1327112 | tf_op jit(solution)/shard_map/while/body/eval_jaxpr/ppermute | solution.py:34
  104.2 7.2 %collective-permute-done = bf16[4,144,384]{2,1,0:T(8,128)(2,1)S(1)} collective-permute-done((bf16[4,144,384]{2,1,0:T(8,128)(2,1)S(1)}, bf16[4,144,384]{2,1,0:T(8,128)(2,1)S(1)}, u32[]{:S(2)}, u32[]{:S(2)}) %collective-permute-start) | collective-permute-done | bytes 442400 | tf_op jit(solution)/shard_map/while/body/eval_jaxpr/ppermute | solution.py:34
  121.9 5.7 %collective-permute-start.1 = (bf16[4,144,384]{2,1,0:T(8,128)(2,1)S(1)}, bf16[4,144,384]{2,1,0:T(8,128)(2,1)S(1)}, u32[]{:S(2)}, u32[]{:S(2)}) collective-permute-start(bf16[4,144,384]{2,1,0:T(8,128)(2,1)S(1)} %get-tuple-element.271), channel_id=1, source_target_pairs={{4,0},{5,1},{6,2},{7,3},{8,4},{9,5},{10,6},{11,7},{12,8},{13,9},{1... | collective-permute-start | bytes 1327112 | tf_op jit(solution)/shard_map/while/body/eval_jaxpr/ppermute | solution.py:34
  127.7 5.5 %collective-permute-done = bf16[4,144,384]{2,1,0:T(8,128)(2,1)S(1)} collective-permute-done((bf16[4,144,384]{2,1,0:T(8,128)(2,1)S(1)}, bf16[4,144,384]{2,1,0:T(8,128)(2,1)S(1)}, u32[]{:S(2)}, u32[]{:S(2)}) %collective-permute-start) | collective-permute-done | bytes 442400 | tf_op jit(solution)/shard_map/while/body/eval_jaxpr/ppermute | solution.py:34
  133.2 6.2 %collective-permute-done.1 = bf16[4,144,384]{2,1,0:T(8,128)(2,1)S(1)} collective-permute-done((bf16[4,144,384]{2,1,0:T(8,128)(2,1)S(1)}, bf16[4,144,384]{2,1,0:T(8,128)(2,1)S(1)}, u32[]{:S(2)}, u32[]{:S(2)}) %collective-permute-start.1) | collective-permute-done | bytes 442400 | tf_op jit(solution)/shard_map/while/body/eval_jaxpr/ppermute | solution.py:34
  146.7 3.9 %collective-permute-start.1 = (bf16[4,144,384]{2,1,0:T(8,128)(2,1)S(1)}, bf16[4,144,384]{2,1,0:T(8,128)(2,1)S(1)}, u32[]{:S(2)}, u32[]{:S(2)}) collective-permute-start(bf16[4,144,384]{2,1,0:T(8,128)(2,1)S(1)} %get-tuple-element.271), channel_id=1, source_target_pairs={{4,0},{5,1},{6,2},{7,3},{8,4},{9,5},{10,6},{11,7},{12,8},{13,9},{1... | collective-permute-start | bytes 1327112 | tf_op jit(solution)/shard_map/while/body/eval_jaxpr/ppermute | solution.py:34
  154.4 9.2 %collective-permute-done.1 = bf16[4,144,384]{2,1,0:T(8,128)(2,1)S(1)} collective-permute-done((bf16[4,144,384]{2,1,0:T(8,128)(2,1)S(1)}, bf16[4,144,384]{2,1,0:T(8,128)(2,1)S(1)}, u32[]{:S(2)}, u32[]{:S(2)}) %collective-permute-start.1) | collective-permute-done | bytes 442400 | tf_op jit(solution)/shard_map/while/body/eval_jaxpr/ppermute | solution.py:34
  167.3 4.3 %collective-permute-start = (bf16[4,144,384]{2,1,0:T(8,128)(2,1)S(1)}, bf16[4,144,384]{2,1,0:T(8,128)(2,1)S(1)}, u32[]{:S(2)}, u32[]{:S(2)}) collective-permute-start(bf16[4,144,384]{2,1,0:T(8,128)(2,1)S(1)} %get-tuple-element.270), channel_id=1, source_target_pairs={{60,0},{61,1},{62,2},{63,3},{0,4},{1,5},{2,6},{3,7},{4,8},{5,9},{6... | collective-permute-start | bytes 1327112 | tf_op jit(solution)/shard_map/while/body/eval_jaxpr/ppermute | solution.py:34
  178.5 7.3 %collective-permute-done.1 = bf16[4,144,384]{2,1,0:T(8,128)(2,1)S(1)} collective-permute-done((bf16[4,144,384]{2,1,0:T(8,128)(2,1)S(1)}, bf16[4,144,384]{2,1,0:T(8,128)(2,1)S(1)}, u32[]{:S(2)}, u32[]{:S(2)}) %collective-permute-start.1) | collective-permute-done | bytes 442400 | tf_op jit(solution)/shard_map/while/body/eval_jaxpr/ppermute | solution.py:34
  200.9 5.8 %collective-permute-done.1 = bf16[4,144,384]{2,1,0:T(8,128)(2,1)S(1)} collective-permute-done((bf16[4,144,384]{2,1,0:T(8,128)(2,1)S(1)}, bf16[4,144,384]{2,1,0:T(8,128)(2,1)S(1)}, u32[]{:S(2)}, u32[]{:S(2)}) %collective-permute-start.1) | collective-permute-done | bytes 442400 | tf_op jit(solution)/shard_map/while/body/eval_jaxpr/ppermute | solution.py:34
  213.7 4.1 %collective-permute-start.1 = (bf16[4,144,384]{2,1,0:T(8,128)(2,1)S(1)}, bf16[4,144,384]{2,1,0:T(8,128)(2,1)S(1)}, u32[]{:S(2)}, u32[]{:S(2)}) collective-permute-start(bf16[4,144,384]{2,1,0:T(8,128)(2,1)S(1)} %get-tuple-element.271), channel_id=1, source_target_pairs={{4,0},{5,1},{6,2},{7,3},{8,4},{9,5},{10,6},{11,7},{12,8},{13,9},{1... | collective-permute-start | bytes 1327112 | tf_op jit(solution)/shard_map/while/body/eval_jaxpr/ppermute | solution.py:34
  217.9 3.7 %collective-permute-done = bf16[4,144,384]{2,1,0:T(8,128)(2,1)S(1)} collective-permute-done((bf16[4,144,384]{2,1,0:T(8,128)(2,1)S(1)}, bf16[4,144,384]{2,1,0:T(8,128)(2,1)S(1)}, u32[]{:S(2)}, u32[]{:S(2)}) %collective-permute-start) | collective-permute-done | bytes 442400 | tf_op jit(solution)/shard_map/while/body/eval_jaxpr/ppermute | solution.py:34
  221.7 5.1 %collective-permute-done.1 = bf16[4,144,384]{2,1,0:T(8,128)(2,1)S(1)} collective-permute-done((bf16[4,144,384]{2,1,0:T(8,128)(2,1)S(1)}, bf16[4,144,384]{2,1,0:T(8,128)(2,1)S(1)}, u32[]{:S(2)}, u32[]{:S(2)}) %collective-permute-start.1) | collective-permute-done | bytes 442400 | tf_op jit(solution)/shard_map/while/body/eval_jaxpr/ppermute | solution.py:34
  233.3 8.4 %collective-permute-done.2 = bf16[4,144,384]{2,1,0:T(8,128)(2,1)S(1)} collective-permute-done((bf16[4,144,384]{2,1,0:T(8,128)(2,1)S(1)}, bf16[4,144,384]{2,1,0:T(8,128)(2,1)S(1)}, u32[]{:S(2)}, u32[]{:S(2)}) %collective-permute-start.2) | collective-permute-done | bytes 442400 | tf_op jit(solution)/shard_map/ppermute | solution.py:34
  247.0 34.6 %all_to_all.30 = bf16[2,144,384]{2,0,1:T(2,128)(2,1)S(1)} all-to-all(bf16[2,144,384]{2,0,1:T(2,128)(2,1)S(1)} %copy.156), channel_id=1, replica_groups=mesh['head'=8,'blk'=64] {'head'}, dimensions={1} | all-to-all | bytes 442368 | tf_op jit(solution)/shard_map/all_to_all | solution.py:21
  (244 shorter events, 88.4 us)
Async XLA Ops:
  21.5 28.5 %all-to-all-start = ((bf16[8,2,20736]{2,1,0:T(2,128)(2,1)}), bf16[8,2,20736]{2,1,0:T(2,128)(2,1)S(1)}, u32[]{:S(2)}, u32[]{:S(2)}) async-start(bf16[8,2,20736]{2,1,0:T(2,128)(2,1)} %reshape.168), calls=%async_computation | async-start | bytes 1327104 | tf_op jit(solution)/shard_map/all_to_all | solution.py:21
  58.1 7.3 %copy-start.2 = (f32[128]{0:T(128)S(1)}, f32[128]{0:T(128)}, u32[]{:S(2)}) copy-start(f32[128]{0:T(128)} %param.17) | copy-start | bytes 1540
  64.5 3.2 %copy-start.3 = (f32[128]{0:T(128)S(1)}, f32[128]{0:T(128)}, u32[]{:S(2)}) copy-start(f32[128]{0:T(128)} %param.16) | copy-start | bytes 1540
  66.8 0.9 copy-start
  68.6 0.7 copy-start.1
  69.4 18.4 %collective-permute-start = (bf16[4,144,384]{2,1,0:T(8,128)(2,1)S(1)}, bf16[4,144,384]{2,1,0:T(8,128)(2,1)S(1)}, u32[]{:S(2)}, u32[]{:S(2)}) collective-permute-start(bf16[4,144,384]{2,1,0:T(8,128)(2,1)S(1)} %get-tuple-element.270), channel_id=1, source_target_pairs={{60,0},{61,1},{62,2},{63,3},{0,4},{1,5},{2,6},{3,7},{4,8},{5,9},{6... | collective-permute-start | bytes 1327112 | tf_op jit(solution)/shard_map/while/body/eval_jaxpr/ppermute | solution.py:34
  71.3 18.7 %collective-permute-start.1 = (bf16[4,144,384]{2,1,0:T(8,128)(2,1)S(1)}, bf16[4,144,384]{2,1,0:T(8,128)(2,1)S(1)}, u32[]{:S(2)}, u32[]{:S(2)}) collective-permute-start(bf16[4,144,384]{2,1,0:T(8,128)(2,1)S(1)} %get-tuple-element.271), channel_id=1, source_target_pairs={{4,0},{5,1},{6,2},{7,3},{8,4},{9,5},{10,6},{11,7},{12,8},{13,9},{1... | collective-permute-start | bytes 1327112 | tf_op jit(solution)/shard_map/while/body/eval_jaxpr/ppermute | solution.py:34
  93.8 17.6 %collective-permute-start = (bf16[4,144,384]{2,1,0:T(8,128)(2,1)S(1)}, bf16[4,144,384]{2,1,0:T(8,128)(2,1)S(1)}, u32[]{:S(2)}, u32[]{:S(2)}) collective-permute-start(bf16[4,144,384]{2,1,0:T(8,128)(2,1)S(1)} %get-tuple-element.270), channel_id=1, source_target_pairs={{60,0},{61,1},{62,2},{63,3},{0,4},{1,5},{2,6},{3,7},{4,8},{5,9},{6... | collective-permute-start | bytes 1327112 | tf_op jit(solution)/shard_map/while/body/eval_jaxpr/ppermute | solution.py:34
  96.2 18.8 %collective-permute-start.1 = (bf16[4,144,384]{2,1,0:T(8,128)(2,1)S(1)}, bf16[4,144,384]{2,1,0:T(8,128)(2,1)S(1)}, u32[]{:S(2)}, u32[]{:S(2)}) collective-permute-start(bf16[4,144,384]{2,1,0:T(8,128)(2,1)S(1)} %get-tuple-element.271), channel_id=1, source_target_pairs={{4,0},{5,1},{6,2},{7,3},{8,4},{9,5},{10,6},{11,7},{12,8},{13,9},{1... | collective-permute-start | bytes 1327112 | tf_op jit(solution)/shard_map/while/body/eval_jaxpr/ppermute | solution.py:34
  118.8 14.3 %collective-permute-start = (bf16[4,144,384]{2,1,0:T(8,128)(2,1)S(1)}, bf16[4,144,384]{2,1,0:T(8,128)(2,1)S(1)}, u32[]{:S(2)}, u32[]{:S(2)}) collective-permute-start(bf16[4,144,384]{2,1,0:T(8,128)(2,1)S(1)} %get-tuple-element.270), channel_id=1, source_target_pairs={{60,0},{61,1},{62,2},{63,3},{0,4},{1,5},{2,6},{3,7},{4,8},{5,9},{6... | collective-permute-start | bytes 1327112 | tf_op jit(solution)/shard_map/while/body/eval_jaxpr/ppermute | solution.py:34
  121.9 17.5 %collective-permute-start.1 = (bf16[4,144,384]{2,1,0:T(8,128)(2,1)S(1)}, bf16[4,144,384]{2,1,0:T(8,128)(2,1)S(1)}, u32[]{:S(2)}, u32[]{:S(2)}) collective-permute-start(bf16[4,144,384]{2,1,0:T(8,128)(2,1)S(1)} %get-tuple-element.271), channel_id=1, source_target_pairs={{4,0},{5,1},{6,2},{7,3},{8,4},{9,5},{10,6},{11,7},{12,8},{13,9},{1... | collective-permute-start | bytes 1327112 | tf_op jit(solution)/shard_map/while/body/eval_jaxpr/ppermute | solution.py:34
  143.2 11.2 %collective-permute-start = (bf16[4,144,384]{2,1,0:T(8,128)(2,1)S(1)}, bf16[4,144,384]{2,1,0:T(8,128)(2,1)S(1)}, u32[]{:S(2)}, u32[]{:S(2)}) collective-permute-start(bf16[4,144,384]{2,1,0:T(8,128)(2,1)S(1)} %get-tuple-element.270), channel_id=1, source_target_pairs={{60,0},{61,1},{62,2},{63,3},{0,4},{1,5},{2,6},{3,7},{4,8},{5,9},{6... | collective-permute-start | bytes 1327112 | tf_op jit(solution)/shard_map/while/body/eval_jaxpr/ppermute | solution.py:34
  146.7 16.9 %collective-permute-start.1 = (bf16[4,144,384]{2,1,0:T(8,128)(2,1)S(1)}, bf16[4,144,384]{2,1,0:T(8,128)(2,1)S(1)}, u32[]{:S(2)}, u32[]{:S(2)}) collective-permute-start(bf16[4,144,384]{2,1,0:T(8,128)(2,1)S(1)} %get-tuple-element.271), channel_id=1, source_target_pairs={{4,0},{5,1},{6,2},{7,3},{8,4},{9,5},{10,6},{11,7},{12,8},{13,9},{1... | collective-permute-start | bytes 1327112 | tf_op jit(solution)/shard_map/while/body/eval_jaxpr/ppermute | solution.py:34
  167.3 11.2 %collective-permute-start = (bf16[4,144,384]{2,1,0:T(8,128)(2,1)S(1)}, bf16[4,144,384]{2,1,0:T(8,128)(2,1)S(1)}, u32[]{:S(2)}, u32[]{:S(2)}) collective-permute-start(bf16[4,144,384]{2,1,0:T(8,128)(2,1)S(1)} %get-tuple-element.270), channel_id=1, source_target_pairs={{60,0},{61,1},{62,2},{63,3},{0,4},{1,5},{2,6},{3,7},{4,8},{5,9},{6... | collective-permute-start | bytes 1327112 | tf_op jit(solution)/shard_map/while/body/eval_jaxpr/ppermute | solution.py:34
  171.6 14.3 %collective-permute-start.1 = (bf16[4,144,384]{2,1,0:T(8,128)(2,1)S(1)}, bf16[4,144,384]{2,1,0:T(8,128)(2,1)S(1)}, u32[]{:S(2)}, u32[]{:S(2)}) collective-permute-start(bf16[4,144,384]{2,1,0:T(8,128)(2,1)S(1)} %get-tuple-element.271), channel_id=1, source_target_pairs={{4,0},{5,1},{6,2},{7,3},{8,4},{9,5},{10,6},{11,7},{12,8},{13,9},{1... | collective-permute-start | bytes 1327112 | tf_op jit(solution)/shard_map/while/body/eval_jaxpr/ppermute | solution.py:34
  189.6 11.2 %collective-permute-start = (bf16[4,144,384]{2,1,0:T(8,128)(2,1)S(1)}, bf16[4,144,384]{2,1,0:T(8,128)(2,1)S(1)}, u32[]{:S(2)}, u32[]{:S(2)}) collective-permute-start(bf16[4,144,384]{2,1,0:T(8,128)(2,1)S(1)} %get-tuple-element.270), channel_id=1, source_target_pairs={{60,0},{61,1},{62,2},{63,3},{0,4},{1,5},{2,6},{3,7},{4,8},{5,9},{6... | collective-permute-start | bytes 1327112 | tf_op jit(solution)/shard_map/while/body/eval_jaxpr/ppermute | solution.py:34
  193.3 13.3 %collective-permute-start.1 = (bf16[4,144,384]{2,1,0:T(8,128)(2,1)S(1)}, bf16[4,144,384]{2,1,0:T(8,128)(2,1)S(1)}, u32[]{:S(2)}, u32[]{:S(2)}) collective-permute-start(bf16[4,144,384]{2,1,0:T(8,128)(2,1)S(1)} %get-tuple-element.271), channel_id=1, source_target_pairs={{4,0},{5,1},{6,2},{7,3},{8,4},{9,5},{10,6},{11,7},{12,8},{13,9},{1... | collective-permute-start | bytes 1327112 | tf_op jit(solution)/shard_map/while/body/eval_jaxpr/ppermute | solution.py:34
  210.5 11.2 %collective-permute-start = (bf16[4,144,384]{2,1,0:T(8,128)(2,1)S(1)}, bf16[4,144,384]{2,1,0:T(8,128)(2,1)S(1)}, u32[]{:S(2)}, u32[]{:S(2)}) collective-permute-start(bf16[4,144,384]{2,1,0:T(8,128)(2,1)S(1)} %get-tuple-element.270), channel_id=1, source_target_pairs={{60,0},{61,1},{62,2},{63,3},{0,4},{1,5},{2,6},{3,7},{4,8},{5,9},{6... | collective-permute-start | bytes 1327112 | tf_op jit(solution)/shard_map/while/body/eval_jaxpr/ppermute | solution.py:34
  213.7 13.0 %collective-permute-start.1 = (bf16[4,144,384]{2,1,0:T(8,128)(2,1)S(1)}, bf16[4,144,384]{2,1,0:T(8,128)(2,1)S(1)}, u32[]{:S(2)}, u32[]{:S(2)}) collective-permute-start(bf16[4,144,384]{2,1,0:T(8,128)(2,1)S(1)} %get-tuple-element.271), channel_id=1, source_target_pairs={{4,0},{5,1},{6,2},{7,3},{8,4},{9,5},{10,6},{11,7},{12,8},{13,9},{1... | collective-permute-start | bytes 1327112 | tf_op jit(solution)/shard_map/while/body/eval_jaxpr/ppermute | solution.py:34
  230.6 11.2 %collective-permute-start.2 = (bf16[4,144,384]{2,1,0:T(8,128)(2,1)S(1)}, bf16[4,144,384]{2,1,0:T(8,128)(2,1)S(1)}, u32[]{:S(2)}, u32[]{:S(2)}) collective-permute-start(bf16[4,144,384]{2,1,0:T(8,128)(2,1)S(1)} %get-tuple-element.61), channel_id=1, source_target_pairs={{60,0},{61,1},{62,2},{63,3},{0,4},{1,5},{2,6},{3,7},{4,8},{5,9},{6... | collective-permute-start | bytes 1327112 | tf_op jit(solution)/shard_map/ppermute | solution.py:34
where the time goes:
time: 285 us; the launch traced here: 283 us
  waiting for transfers between devices  101 us (35%)
  starting transfers between devices  72.4 us (25%)
  local copies, waits for them, and re-layouts  44.1 us (15%)
  blocking collectives  34.6 us (12%)
  matrix products  23.3 us (8%)
  other arithmetic  6.41 us (2%)
    ppermute x15, waiting for transfers between devices, passed_along(): return lax.ppermute(block, axis, route)  83.3 us
    ppermute x15, starting transfers between devices, passed_along(): return lax.ppermute(block, axis, route)  62.1 us
    all_to_all x1, blocking collectives, in_one_piece(): lax.all_to_all(both, axis, split_axis=split_dim, concat_axis=concat_dim,...  34.6 us
    unnamed x20, local copies, waits for them, and re-layouts  22.4 us
    all_to_all x1, waiting for transfers between devices, in_one_piece(): lax.all_to_all(both, axis, split_axis=split_dim, concat_axis=concat_dim,...  17.2 us
    dot_general x8, matrix products, absorb_segment(): jnp.einsum('qhd,khd->hqk', query_pair, key_pair, preferred_element_type=j...  11 us
    all_to_all x1, starting transfers between devices, in_one_piece(): lax.all_to_all(both, axis, split_axis=split_dim, concat_axis=concat_dim,...  10.3 us
    concatenate x3, local copies, waits for them, and re-layouts, in_one_piece(): both = jnp.concatenate(arrays, axis=along)  6.88 us
  transfers between devices with their start and end apart: 16, of which 16 were waited for; matrix products, arithmetic and copies ran while one was open for 0% of the time, Pallas kernels for 0%

commit v1 on v0

v1 whole, which is shorter than its diff:
```python
import math

import jax
import jax.numpy as jnp
from jax import lax
from jax.experimental import pallas as pl
from jax.experimental.pallas import tpu as pltpu
from jax.sharding import PartitionSpec as P

HD = 128
TXT = 512
GRID_W = 64
IMAGES = 4
RING = 8
PART = 18
BLOCK = RING * PART
STREAMS = 3
PIECES = 8
ITEMS = STREAMS * PIECES
LAG = 1

EPSILON = 1e-06
THETA = 10000.0
SCALE = 1.0 / math.sqrt(HD)
MESH = pl.DeviceIdType.MESH


def rows_at(slot):
    return pl.ds(pl.multiple_of(slot * BLOCK, 16), BLOCK)


def columns_at(head):
    return pl.ds(pl.multiple_of(head * HD, HD), HD)


def kernel(
    query_ref,
    key_ref,
    value_ref,
    query_tan_ref,
    key_tan_ref,
    value_tan_ref,
    query_gain_ref,
    key_gain_ref,
    out_ref,
    out_tan_ref,
    packed,
    landed,
    queries,
    store,
    peak,
    total,
    drift,
    summed,
    result,
    returned,
    kv_send,
    kv_recv,
    q_send,
    q_recv,
    ag_send,
    ag_recv,
    back_send,
    back_recv,
):
    head = lax.axis_index("head")
    blk = lax.axis_index("blk")
    core = head % 2
    x = blk % IMAGES
    y = (head // 2) * 2 + (blk // IMAGES) % 2
    z = blk // (2 * IMAGES)

    def device(yy, zz, cc):
        return {"head": (yy // 2) * 2 + cc, "blk": (zz * 2 + yy % 2) * IMAGES + x}

    def spread(stream, hops):
        flip = stream % 2
        return device((y + hops * (1 - flip)) % RING, (z + hops * flip) % RING, core)

    def along(stream, hops):
        flip = stream % 2
        return device((y + hops * flip) % RING, (z + hops * (1 - flip)) % RING, core)

    partner = device(y, z, 1 - core)

    def head_of(stream, hops):
        if stream == 1:
            return 2 * RING + (z + hops) % RING
        return 2 * ((y + hops) % RING) + stream // 2

    barrier = pltpu.get_barrier_semaphore()

    def greet(k, carry):
        pl.semaphore_signal(barrier, inc=1, device_id=spread(0, k), device_id_type=MESH)
        pl.semaphore_signal(barrier, inc=1, device_id=spread(1, k), device_id_type=MESH)
        return carry

    lax.fori_loop(1, RING, greet, 0)
    pl.semaphore_signal(barrier, inc=1, device_id=partner, device_id_type=MESH)

    place = blk // IMAGES
    token = place * BLOCK + head * PART + lax.broadcasted_iota(jnp.int32, (PART, HD), 0)
    lane = lax.broadcasted_iota(jnp.int32, (PART, HD), 1)
    pair = lax.shift_right_logical(lane, 1)
    patch = jnp.maximum(token - TXT, 0)
    row_id = lax.shift_right_logical(patch, 6).astype(jnp.float32)
    column_id = (patch & (GRID_W - 1)).astype(jnp.float32)
    in_row = pair < 36
    step = jnp.where(in_row, pair - 8, pair - 36).astype(jnp.float32)
    frequency = jnp.exp(-math.log(THETA) * (step * (2.0 / 56)))
    angle = jnp.where(in_row, row_id, column_id) * frequency
    angle = jnp.where(pair < 8, 0.0, angle)
    odd = (lane & 1) == 1
    cosine = jnp.cos(angle)
    sine = jnp.sin(angle)
    sine = jnp.where(odd, sine, -sine)

    def rotate(v):
        swapped = jnp.where(odd, pltpu.roll(v, 1, 1), pltpu.roll(v, HD - 1, 1))
        return v * cosine + swapped * sine

    def normalize(raw, tangent, gain):
        values = raw.astype(jnp.float32)
        motion = tangent.astype(jnp.float32)
        inverse = lax.rsqrt(jnp.mean(values * values, axis=-1, keepdims=True) + EPSILON)
        coupling = jnp.mean(values * motion, axis=-1, keepdims=True)
        normed = values * inverse * gain
        normed_dot = gain * (
            motion * inverse - values * (inverse * inverse * inverse * coupling)
        )
        return rotate(normed).astype(jnp.bfloat16), rotate(normed_dot).astype(jnp.bfloat16)

    query_gain = query_gain_ref[...]
    key_gain = key_gain_ref[...]

    def pack(k, carry):
        for stream in range(STREAMS):
            cols = columns_at(head_of(stream, k))
            query_hat, query_dot = normalize(
                query_ref[0, :, cols], query_tan_ref[0, :, cols], query_gain
            )
            key_hat, key_dot = normalize(
                key_ref[0, :, cols], key_tan_ref[0, :, cols], key_gain
            )
            arrays = (
                query_hat,
                query_dot,
                key_hat,
                key_dot,
                value_ref[0, :, cols],
                value_tan_ref[0, :, cols],
            )
            for a, v in enumerate(arrays):
                packed[k, stream, a, 0:8] = v[0:16].reshape(8, 2, HD)
                packed[k, stream, a, 8] = v[16:18]
        return carry

    lax.fori_loop(0, RING, pack, 0)
    for stream in range(STREAMS):
        landed[stream, :, 0:9] = packed[0, stream]

    pl.semaphore_wait(barrier, 2 * RING - 1)

    def kv_copy(stream, k):
        return pltpu.make_async_remote_copy(
            src_ref=packed.at[k, stream, pl.ds(2, 4)],
            dst_ref=landed.at[stream, pl.ds(2, 4), pl.ds(k * 9, 9)],
            send_sem=kv_send.at[stream, k],
            recv_sem=kv_recv.at[stream, k],
            device_id=spread(stream, k),
            device_id_type=MESH,
        )

    def q_copy(stream, k):
        return pltpu.make_async_remote_copy(
            src_ref=packed.at[k, stream, pl.ds(0, 2)],
            dst_ref=landed.at[stream, pl.ds(0, 2), pl.ds(k * 9, 9)],
            send_sem=q_send.at[stream, k],
            recv_sem=q_recv.at[stream, k],
            device_id=spread(stream, k),
            device_id_type=MESH,
        )

    def for_peers(action):
        def one(k, carry):
            action(k)
            return carry

        lax.fori_loop(1, RING, one, 0)

    for stream in range(STREAMS):
        for_peers(lambda k: kv_copy(stream, k).start())
    for stream in range(STREAMS):
        for_peers(lambda k: q_copy(stream, k).start())

    def ag_copy(stream, source, target, pair_of, to):
        return pltpu.make_async_remote_copy(
            src_ref=store.at[stream, pl.ds(2 * pair_of, 2), rows_at(source)],
            dst_ref=store.at[stream, pl.ds(2 * pair_of, 2), rows_at(target)],
            send_sem=ag_send.at[stream, target, pair_of],
            recv_sem=ag_recv.at[stream, target, pair_of],
            device_id=to,
            device_id_type=MESH,
        )

    def arrived(stream, slot, pair_of):
        ag_copy(stream, slot, slot, pair_of, partner).wait_recv()

    for stream in range(STREAMS):
        for_peers(lambda k: kv_copy(stream, k).wait_recv())
        for a in range(4):
            store[stream, a, 0:BLOCK] = landed.at[stream, 2 + a].reshape(BLOCK, HD)[...]
        for pair_of in range(2):
            ag_copy(stream, 0, 2, pair_of, along(stream, 1)).start()
            ag_copy(stream, 0, 4, pair_of, along(stream, RING - 1)).start()
        for pair_of in range(2):
            ag_copy(stream, 0, 1, pair_of, partner).start()

    for stream in range(STREAMS):
        for_peers(lambda k: q_copy(stream, k).wait_recv())
        query_hat = landed.at[stream, 0].reshape(BLOCK, HD)[...]
        query_dot = landed.at[stream, 1].reshape(BLOCK, HD)[...]
        queries[stream, :, 0:HD] = query_dot
        queries[stream, :, HD : 2 * HD] = query_hat
        peak[stream] = jnp.full((BLOCK, 1), -jnp.inf, jnp.float32)
        total[stream] = jnp.zeros((BLOCK, 1), jnp.float32)
        drift[stream] = jnp.zeros((BLOCK, 1), jnp.float32)
        summed[stream] = jnp.zeros((BLOCK, 2 * HD), jnp.float32)

    def pass_on(item):
        stream = item % STREAMS
        piece = item // STREAMS
        slot = 2 * piece
        onward = along(stream, 1 + (piece + 1) % 2 * (RING - 2))
        for pair_of in range(2):
            arrived(stream, slot, pair_of)

            @pl.when(piece <= 4)
            def _():
                ag_copy(stream, slot, slot + 4, pair_of, onward).start()

            @pl.when(piece == 5 + pair_of)
            def _():
                ag_copy(stream, slot, 14, pair_of, onward).start()

            ag_copy(stream, slot, slot + 1, pair_of, partner).start()

    def absorb(item):
        stream = item % STREAMS
        piece = item // STREAMS
        for pair_of in range(2):
            arrived(stream, 2 * piece + 1, pair_of)
        rows = pl.ds(pl.multiple_of(piece * (2 * BLOCK), 32), 2 * BLOCK)
        query_pair = queries[stream]
        query_hat = query_pair[:, HD:]
        key = store[stream, 0, rows]
        key_pair = jnp.concatenate([key, store[stream, 1, rows]], axis=1)
        value = store[stream, 2, rows]
        value_pair = jnp.concatenate([value, store[stream, 3, rows]], axis=1)
        contract = (((1,), (1,)), ((), ()))
        scores = (
            lax.dot_general(query_hat, key, contract, preferred_element_type=jnp.float32)
            * SCALE
        )
        scores_dot = (
            lax.dot_general(
                query_pair, key_pair, contract, preferred_element_type=jnp.float32
            )
            * SCALE
        )
        old_peak = peak[stream]
        new_peak = jnp.maximum(old_peak, jnp.max(scores, axis=1, keepdims=True))
        rescale = jnp.exp(old_peak - new_peak)
        weights = jnp.exp(scores - new_peak)
        product = weights * scores_dot
        peak[stream] = new_peak
        total[stream] = total[stream] * rescale + jnp.sum(weights, axis=1, keepdims=True)
        drift[stream] = drift[stream] * rescale + jnp.sum(product, axis=1, keepdims=True)
        low_weights = weights.astype(jnp.bfloat16)
        low_product = product.astype(jnp.bfloat16)
        first = jnp.dot(low_weights, value_pair, preferred_element_type=jnp.float32)
        second = jnp.dot(low_product, value, preferred_element_type=jnp.float32)
        summed[stream, :, 0:HD] = summed[stream, :, 0:HD] * rescale + first[:, 0:HD]
        summed[stream, :, HD:] = (
            summed[stream, :, HD:] * rescale + first[:, HD:] + second
        )

    def advance(item, carry):
        @pl.when((item >= STREAMS) & (item < ITEMS))
        def _():
            pass_on(item)

        absorb(item - LAG)
        return carry

    lax.fori_loop(LAG, ITEMS + LAG, advance, 0)

    def back_copy(stream, k):
        return pltpu.make_async_remote_copy(
            src_ref=result.at[stream, :, pl.ds(k * 9, 9)],
            dst_ref=returned.at[k, stream],
            send_sem=back_send.at[stream, k],
            recv_sem=back_recv.at[stream, k],
            device_id=spread(stream, RING - k),
            device_id_type=MESH,
        )

    for stream in range(STREAMS):
        inverse = 1.0 / total[stream]
        base = summed[stream, :, 0:HD]
        attended = base * inverse
        tangent = (summed[stream, :, HD:] - drift[stream] * inverse * base) * inverse
        result.at[stream, 0].reshape(BLOCK, HD)[...] = attended.astype(jnp.bfloat16)
        result.at[stream, 1].reshape(BLOCK, HD)[...] = tangent.astype(jnp.bfloat16)
        for_peers(lambda k: back_copy(stream, k).start())

    def unpack(stream, k):
        cols = columns_at(head_of(stream, k))
        for a, ref in enumerate((out_ref, out_tan_ref)):
            ref[0, 0:16, cols] = returned[k, stream, a, 0:8].reshape(16, HD)
            ref[0, 16:18, cols] = returned[k, stream, a, 8]

    for stream in range(STREAMS):
        returned[0, stream] = result[stream, :, 0:9]
        unpack(stream, 0)

    for stream in range(STREAMS):

        def finish(k):
            back_copy(stream, k).wait_recv()
            unpack(stream, k)

        for_peers(finish)

    for stream in range(STREAMS):

        def settle(k):
            kv_copy(stream, k).wait_send()
            q_copy(stream, k).wait_send()
            back_copy(stream, k).wait_send()

        for_peers(settle)

        def settle_ring(slot, carry):
            for pair_of in range(2):
                ag_copy(stream, slot, slot, pair_of, partner).wait_send()
            return carry

        lax.fori_loop(1, 2 * PIECES, settle_ring, 0)


def local(*operands):
    arrays, gains = operands[:6], operands[6:]
    shape = jax.ShapeDtypeStruct((1, PART, arrays[0].shape[2]), jnp.bfloat16)
    vmem = pl.BlockSpec(memory_space=pltpu.VMEM)
    dma = pltpu.SemaphoreType.DMA
    bf16, f32 = jnp.bfloat16, jnp.float32
    out = pl.pallas_call(
        kernel,
        out_shape=(shape, shape),
        in_specs=[vmem] * 8,
        out_specs=(vmem, vmem),
        scratch_shapes=[
            pltpu.VMEM((RING, STREAMS, 6, 9, 2, HD), bf16),
            pltpu.VMEM((STREAMS, 6, 72, 2, HD), bf16),
            pltpu.VMEM((STREAMS, BLOCK, 2 * HD), bf16),
            pltpu.VMEM((STREAMS, 4, 2 * PIECES * BLOCK, HD), bf16),
            pltpu.VMEM((STREAMS, BLOCK, 1), f32),
            pltpu.VMEM((STREAMS, BLOCK, 1), f32),
            pltpu.VMEM((STREAMS, BLOCK, 1), f32),
            pltpu.VMEM((STREAMS, BLOCK, 2 * HD), f32),
            pltpu.VMEM((STREAMS, 2, 72, 2, HD), bf16),
            pltpu.VMEM((RING, STREAMS, 2, 9, 2, HD), bf16),
            dma((STREAMS, RING)),
            dma((STREAMS, RING)),
            dma((STREAMS, RING)),
            dma((STREAMS, RING)),
            dma((STREAMS, 2 * PIECES, 2)),
            dma((STREAMS, 2 * PIECES, 2)),
            dma((STREAMS, RING)),
            dma((STREAMS, RING)),
        ],
        compiler_params=pltpu.CompilerParams(
            collective_id=0,
            has_side_effects=True,
            vmem_limit_bytes=40 * 1024 * 1024,
        ),
    )(*arrays, *(g.reshape(1, HD) for g in gains))
    return out[0], out[1]


def solution(mesh):
    rows = P("blk", "head", None)
    return jax.shard_map(
        local,
        mesh=mesh,
        in_specs=(rows,) * 6 + (P(), P()),
        out_specs=(rows, rows),
        check_vma=False,
    )
```

time: 285 us -> 69.6 us (0.24)
  waiting for transfers between devices: 101 us -> 0 us
  starting transfers between devices: 72.4 us -> 0 us
  Pallas kernels: 0 us -> 61.3 us
  local copies, waits for them, and re-layouts: 44.1 us -> 7.44 us
  blocking collectives: 34.6 us -> 0 us
  matrix products: 23.3 us -> 0 us
  other arithmetic: 6.41 us -> 0 us
    ppermute x15 -> x0, waiting for transfers between devices: 83.3 us -> none  [passed_along(): return lax.ppermute(block, axis, route)]
    ppermute x15 -> x0, starting transfers between devices: 62.1 us -> none  [passed_along(): return lax.ppermute(block, axis, route)]
    pallas_call x0 -> x1, Pallas kernels: none -> 61.3 us  [local(): pl.pallas_call(kernel, out_shape=(shape, shape), in_specs=[vmem] * 8, out...]
    all_to_all x1 -> x0, blocking collectives: 34.6 us -> none  [in_one_piece(): lax.all_to_all(both, axis, split_axis=split_dim, concat_axis=concat_dim,...]
    dot_general x44 -> x0, matrix products: 23.3 us -> none  [the longest x8 11 us: absorb_segment(): jnp.einsum('qhd,khd->hqk', query_pair, key_pair, preferred_element_type=j...]
    all_to_all x1 -> x0, waiting for transfers between devices: 17.2 us -> none  [in_one_piece(): lax.all_to_all(both, axis, split_axis=split_dim, concat_axis=concat_dim,...]
    unnamed x20 -> x18, local copies, waits for them, and re-layouts: 22.4 us -> 7.44 us
    all_to_all x1 -> x0, starting transfers between devices: 10.3 us -> none  [in_one_piece(): lax.all_to_all(both, axis, split_axis=split_dim, concat_axis=concat_dim,...]
  transfers between devices with their start and end apart: 16 -> 0, of which waited for: 16 -> 0; matrix products, arithmetic and copies ran while one was open for 0% -> 0% of each run, Pallas kernels for 0% -> 0%
where the time goes in v1:
time: 69.6 us; the launch traced here: 69.4 us
  Pallas kernels  61.3 us (88%)
  local copies, waits for them, and re-layouts  7.44 us (11%)
    pallas_call x1, Pallas kernels, local(): pl.pallas_call(kernel, out_shape=(shape, shape), in_specs=[vmem] * 8, out...  61.3 us
    unnamed x18, local copies, waits for them, and re-layouts  7.44 us

profile of v1, /device:TPU:1, one launch (start us, length us, event | category | flops | bytes accessed | tf_op | source)
XLA Modules:
  0.0 69.4 jit_solution(12534554577108342188)
XLA Ops:
  0.6 0.0 copy-start.6
  0.6 0.0 copy-start.7
  0.7 0.6 copy-done.6
  1.3 0.0 copy-done.7
  1.3 0.0 copy-start
  1.3 0.9 %copy-done = bf16[1,18,3072]{2,1,0:T(8,128)(2,1)S(1)} copy-done((bf16[1,18,3072]{2,1,0:T(8,128)(2,1)S(1)}, bf16[1,18,3072]{2,1,0:T(8,128)(2,1)}, u32[]{:S(2)}) %copy-start) | copy-done | bytes 110616
  2.2 0.0 copy-start.1
  2.2 0.9 %copy-done.1 = bf16[1,18,3072]{2,1,0:T(8,128)(2,1)S(1)} copy-done((bf16[1,18,3072]{2,1,0:T(8,128)(2,1)S(1)}, bf16[1,18,3072]{2,1,0:T(8,128)(2,1)}, u32[]{:S(2)}) %copy-start.1) | copy-done | bytes 110616
  3.1 0.0 copy-start.2
  3.1 0.9 %copy-done.2 = bf16[1,18,3072]{2,1,0:T(8,128)(2,1)S(1)} copy-done((bf16[1,18,3072]{2,1,0:T(8,128)(2,1)S(1)}, bf16[1,18,3072]{2,1,0:T(8,128)(2,1)}, u32[]{:S(2)}) %copy-start.2) | copy-done | bytes 110616
  4.0 0.0 copy-start.3
  4.0 0.9 %copy-done.3 = bf16[1,18,3072]{2,1,0:T(8,128)(2,1)S(1)} copy-done((bf16[1,18,3072]{2,1,0:T(8,128)(2,1)S(1)}, bf16[1,18,3072]{2,1,0:T(8,128)(2,1)}, u32[]{:S(2)}) %copy-start.3) | copy-done | bytes 110616
  4.9 0.0 copy-start.4
  4.9 0.9 %copy-done.4 = bf16[1,18,3072]{2,1,0:T(8,128)(2,1)S(1)} copy-done((bf16[1,18,3072]{2,1,0:T(8,128)(2,1)S(1)}, bf16[1,18,3072]{2,1,0:T(8,128)(2,1)}, u32[]{:S(2)}) %copy-start.4) | copy-done | bytes 110616
  5.9 0.0 copy-start.5
  5.9 0.9 %copy-done.5 = bf16[1,18,3072]{2,1,0:T(8,128)(2,1)S(1)} copy-done((bf16[1,18,3072]{2,1,0:T(8,128)(2,1)S(1)}, bf16[1,18,3072]{2,1,0:T(8,128)(2,1)}, u32[]{:S(2)}) %copy-start.5) | copy-done | bytes 110616
  6.8 61.3 %shard_map.95 = (bf16[1,18,3072]{2,1,0:T(8,128)(2,1)S(1)}, bf16[1,18,3072]{2,1,0:T(8,128)(2,1)S(1)}) custom-call(bf16[1,18,3072]{2,1,0:T(8,128)(2,1)S(1)} %copy-done, bf16[1,18,3072]{2,1,0:T(8,128)(2,1)S(1)} %copy-done.1, bf16[1,18,3072]{2,1,0:T(8,128)(2,1)S(1)} %copy-done.2, bf16[1,18,3072]{2,1,0:T(8,128)(2,1)S(1)} %copy-done.3, ...), custom_call_target="tpu_custom_call" | custom-call | tf_op jit(solution)/shard_map/pallas_call | solution.py:358
  68.1 0.7 copy.12
  68.7 0.7 copy.13
Async XLA Ops:
  0.6 0.7 copy-start.6
  0.6 0.7 copy-start.7
  1.3 0.9 %copy-start = (bf16[1,18,3072]{2,1,0:T(8,128)(2,1)S(1)}, bf16[1,18,3072]{2,1,0:T(8,128)(2,1)}, u32[]{:S(2)}) copy-start(bf16[1,18,3072]{2,1,0:T(8,128)(2,1)} %query_ref.1) | copy-start | bytes 331780
  2.2 0.9 %copy-start.1 = (bf16[1,18,3072]{2,1,0:T(8,128)(2,1)S(1)}, bf16[1,18,3072]{2,1,0:T(8,128)(2,1)}, u32[]{:S(2)}) copy-start(bf16[1,18,3072]{2,1,0:T(8,128)(2,1)} %key_ref.1) | copy-start | bytes 331780
  3.1 0.9 %copy-start.2 = (bf16[1,18,3072]{2,1,0:T(8,128)(2,1)S(1)}, bf16[1,18,3072]{2,1,0:T(8,128)(2,1)}, u32[]{:S(2)}) copy-start(bf16[1,18,3072]{2,1,0:T(8,128)(2,1)} %value_ref.1) | copy-start | bytes 331780
  4.0 0.9 %copy-start.3 = (bf16[1,18,3072]{2,1,0:T(8,128)(2,1)S(1)}, bf16[1,18,3072]{2,1,0:T(8,128)(2,1)}, u32[]{:S(2)}) copy-start(bf16[1,18,3072]{2,1,0:T(8,128)(2,1)} %query_tan_ref.1) | copy-start | bytes 331780
  4.9 0.9 %copy-start.4 = (bf16[1,18,3072]{2,1,0:T(8,128)(2,1)S(1)}, bf16[1,18,3072]{2,1,0:T(8,128)(2,1)}, u32[]{:S(2)}) copy-start(bf16[1,18,3072]{2,1,0:T(8,128)(2,1)} %key_tan_ref.1) | copy-start | bytes 331780
  5.9 0.9 %copy-start.5 = (bf16[1,18,3072]{2,1,0:T(8,128)(2,1)S(1)}, bf16[1,18,3072]{2,1,0:T(8,128)(2,1)}, u32[]{:S(2)}) copy-start(bf16[1,18,3072]{2,1,0:T(8,128)(2,1)} %value_tan_ref.1) | copy-start | bytes 331780

commit v2 on v1

v2 whole, which is shorter than its diff:
```python
import math

import jax
import jax.numpy as jnp
from jax import lax
from jax.experimental import pallas as pl
from jax.experimental.pallas import tpu as pltpu
from jax.sharding import PartitionSpec as P

HD = 128
TXT = 512
GRID_W = 64
IMAGES = 4
RING = 8
PART = 18
BLOCK = RING * PART
STREAMS = 3
PIECES = 8
PASS, ABSORB = 0, 1
ORDER = (
    (PASS, 1, 0, 1), (PASS, 0, 0, 1), (PASS, 1, 0, 0), (PASS, 0, 0, 0), (ABSORB, 1, 0, 1),
    (PASS, 0, 1, 1), (PASS, 0, 2, 1), (PASS, 2, 0, 1), (PASS, 0, 1, 0), (PASS, 0, 2, 0),
    (PASS, 2, 0, 0), (PASS, 0, 3, 1), (PASS, 0, 4, 1), (ABSORB, 0, 0, 1), (PASS, 2, 1, 1),
    (PASS, 2, 2, 1), (ABSORB, 0, 1, 2), (ABSORB, 2, 0, 1), (PASS, 0, 3, 0), (PASS, 0, 4, 0),
    (PASS, 1, 1, 1), (PASS, 1, 2, 1), (PASS, 2, 1, 0), (PASS, 2, 2, 0), (PASS, 1, 1, 0),
    (PASS, 1, 2, 0), (ABSORB, 0, 3, 2), (PASS, 0, 5, 1), (PASS, 0, 6, 1), (ABSORB, 2, 1, 2),
    (PASS, 1, 3, 1), (PASS, 1, 4, 1), (PASS, 2, 3, 1), (PASS, 2, 4, 1), (ABSORB, 1, 1, 2),
    (PASS, 1, 3, 0), (PASS, 1, 4, 0), (PASS, 0, 5, 0), (PASS, 0, 6, 0), (PASS, 2, 3, 0),
    (PASS, 2, 4, 0), (PASS, 1, 5, 1), (PASS, 1, 6, 1), (ABSORB, 1, 3, 2), (PASS, 2, 5, 1),
    (PASS, 0, 7, 1), (PASS, 1, 5, 0), (PASS, 1, 6, 0), (ABSORB, 0, 5, 2), (PASS, 0, 7, 0),
    (PASS, 2, 6, 1), (ABSORB, 2, 3, 2), (PASS, 1, 7, 1), (PASS, 2, 5, 0), (PASS, 2, 6, 0),
    (ABSORB, 1, 5, 2), (PASS, 1, 7, 0), (ABSORB, 0, 7, 1), (PASS, 2, 7, 1), (ABSORB, 2, 5, 2),
    (ABSORB, 1, 7, 1), (PASS, 2, 7, 0), (ABSORB, 2, 7, 1),
)
QUERY, KEY, VALUE = 0, 1, 2

EPSILON = 1e-06
THETA = 10000.0
SCALE = 1.0 / math.sqrt(HD)
MESH = pl.DeviceIdType.MESH


def rows_at(slot):
    return pl.ds(slot * BLOCK, BLOCK)


def columns_at(head):
    return pl.ds(pl.multiple_of(head * HD, HD), HD)


def kernel(
    query_hbm,
    key_hbm,
    value_hbm,
    query_tan_hbm,
    key_tan_hbm,
    value_tan_hbm,
    query_gain_hbm,
    key_gain_hbm,
    out_ref,
    out_tan_ref,
    inputs,
    gains,
    packed,
    landed,
    queries,
    store,
    peak,
    total,
    drift,
    summed,
    result,
    returned,
    input_sem,
    spread_send,
    spread_recv,
    ring_send,
    ring_recv,
    partner_recv,
    back_send,
    back_recv,
):
    sources = (query_hbm, query_tan_hbm, key_hbm, key_tan_hbm, value_hbm, value_tan_hbm)
    loads = [
        pltpu.make_async_copy(source.at[0], inputs.at[a], input_sem.at[a])
        for a, source in enumerate(sources)
    ]
    for i, source in enumerate((query_gain_hbm, key_gain_hbm)):
        loads.append(pltpu.make_async_copy(source, gains.at[i], input_sem.at[6 + i]))
    for a in (4, 5, 2, 3, 7, 0, 1, 6):
        loads[a].start()

    head = lax.axis_index("head")
    blk = lax.axis_index("blk")
    core = head % 2
    x = blk % IMAGES
    y = (head // 2) * 2 + (blk // IMAGES) % 2
    z = blk // (2 * IMAGES)

    def device(yy, zz, cc):
        return {"head": (yy // 2) * 2 + cc, "blk": (zz * 2 + yy % 2) * IMAGES + x}

    def spread(stream, hops):
        flip = stream % 2
        return device((y + hops * (1 - flip)) % RING, (z + hops * flip) % RING, core)

    def along(stream, hops):
        flip = stream % 2
        return device((y + hops * flip) % RING, (z + hops * (1 - flip)) % RING, core)

    partner = device(y, z, 1 - core)

    def head_of(stream, hops):
        if stream == 1:
            return 2 * RING + (z + hops) % RING
        return 2 * ((y + hops) % RING) + stream // 2

    barrier = pltpu.get_barrier_semaphore()

    def greet(k, carry):
        pl.semaphore_signal(barrier, inc=1, device_id=spread(0, k), device_id_type=MESH)
        pl.semaphore_signal(barrier, inc=1, device_id=spread(1, k), device_id_type=MESH)
        return carry

    lax.fori_loop(1, RING, greet, 0)
    pl.semaphore_signal(barrier, inc=1, device_id=partner, device_id_type=MESH)

    place = blk // IMAGES
    token = place * BLOCK + head * PART + lax.broadcasted_iota(jnp.int32, (PART, HD), 0)
    lane = lax.broadcasted_iota(jnp.int32, (PART, HD), 1)
    pair = lax.shift_right_logical(lane, 1)
    patch = jnp.maximum(token - TXT, 0)
    row_id = lax.shift_right_logical(patch, 6).astype(jnp.float32)
    column_id = (patch & (GRID_W - 1)).astype(jnp.float32)
    in_row = pair < 36
    step = jnp.where(in_row, pair - 8, pair - 36).astype(jnp.float32)
    frequency = jnp.exp(-math.log(THETA) * (step * (2.0 / 56)))
    angle = jnp.where(in_row, row_id, column_id) * frequency
    angle = jnp.where(pair < 8, 0.0, angle)
    odd = (lane & 1) == 1
    cosine = jnp.cos(angle)
    sine = jnp.sin(angle)
    sine = jnp.where(odd, sine, -sine)

    def rotate(v):
        swapped = jnp.where(odd, pltpu.roll(v, 1, 1), pltpu.roll(v, HD - 1, 1))
        return v * cosine + swapped * sine

    def normalize(raw, tangent, gain):
        values = raw.astype(jnp.float32)
        motion = tangent.astype(jnp.float32)
        inverse = lax.rsqrt(jnp.mean(values * values, axis=-1, keepdims=True) + EPSILON)
        coupling = jnp.mean(values * motion, axis=-1, keepdims=True)
        normed = values * inverse * gain
        normed_dot = gain * (
            motion * inverse - values * (inverse * inverse * inverse * coupling)
        )
        return rotate(normed).astype(jnp.bfloat16), rotate(normed_dot).astype(jnp.bfloat16)

    def put(k, stream, a, v):
        packed[k, stream, a, 0:8] = v[0:16].reshape(8, 2, HD)
        packed[k, stream, a, 8] = v[16:18]

    def pack(stream, group):
        def one(k, carry):
            cols = columns_at(head_of(stream, k))
            raw, tangent = inputs[2 * group, :, cols], inputs[2 * group + 1, :, cols]
            if group != VALUE:
                raw, tangent = normalize(raw, tangent, gains[group])
            put(k, stream, 2 * group, raw)
            put(k, stream, 2 * group + 1, tangent)
            return carry

        lax.fori_loop(0, RING, one, 0, unroll=4)
        pair = pl.ds(2 * group, 2)
        landed[stream, pair, 0:9] = packed[0, stream, pair]

    def spread_copy(stream, group, k):
        pair = pl.ds(2 * group, 2)
        return pltpu.make_async_remote_copy(
            src_ref=packed.at[k, stream, pair],
            dst_ref=landed.at[stream, pair, pl.ds(k * 9, 9)],
            send_sem=spread_send,
            recv_sem=spread_recv.at[stream, group],
            device_id=spread(stream, k),
            device_id_type=MESH,
        )

    def send_out(stream, group):
        def one(k, carry):
            spread_copy(stream, group, k).start()
            return carry

        lax.fori_loop(1, RING, one, 0)

    def await_bytes(ref, sem):
        pltpu.make_async_copy(ref, ref, sem).wait()

    for a in (4, 5):
        loads[a].wait()
    for stream in range(STREAMS):
        pack(stream, VALUE)
    for a in (2, 3, 7):
        loads[a].wait()
    for stream in (0, 1):
        pack(stream, KEY)
    pl.semaphore_wait(barrier, 2 * RING - 1)
    for group in (VALUE, KEY):
        for stream in (0, 1):
            send_out(stream, group)
    send_out(2, VALUE)
    pack(2, KEY)
    send_out(2, KEY)
    for a in (0, 1, 6):
        loads[a].wait()
    for stream in (1, 0, 2):
        pack(stream, QUERY)
        send_out(stream, QUERY)

    def ring_copy(stream, source, target, pair_of, to):
        pair = pl.ds(2 * pair_of, 2)
        return pltpu.make_async_remote_copy(
            src_ref=store.at[stream, pair, rows_at(source)],
            dst_ref=store.at[stream, pair, rows_at(target)],
            send_sem=ring_send.at[stream],
            recv_sem=ring_recv.at[stream, target // 2, pair_of],
            device_id=to,
            device_id_type=MESH,
        )

    def hand_over(stream, source, pair_of):
        pair = pl.ds(2 * pair_of, 2)
        return pltpu.make_async_remote_copy(
            src_ref=store.at[stream, pair, rows_at(source)],
            dst_ref=store.at[stream, pair, rows_at(source + 1)],
            send_sem=ring_send.at[stream],
            recv_sem=partner_recv.at[stream, source // 2],
            device_id=partner,
            device_id_type=MESH,
        )

    def begin(stream, pair_of):
        pair = pl.ds(2 * (pair_of + 1), 2)
        await_bytes(
            landed.at[stream, pair, pl.ds(9, 63)], spread_recv.at[stream, pair_of + 1]
        )
        for a in (2 * pair_of, 2 * pair_of + 1):
            store[stream, a, 0:BLOCK] = landed.at[stream, 2 + a].reshape(BLOCK, HD)[...]
        ring_copy(stream, 0, 2, pair_of, along(stream, 1)).start()
        ring_copy(stream, 0, 4, pair_of, along(stream, RING - 1)).start()
        hand_over(stream, 0, pair_of).start()

    def pass_on(stream, piece, pair_of):
        slot = 2 * piece
        await_bytes(
            store.at[stream, pl.ds(2 * pair_of, 2), rows_at(slot)],
            ring_recv.at[stream, piece, pair_of],
        )
        onward = along(stream, 1 if piece % 2 else RING - 1)
        if piece <= 4:
            ring_copy(stream, slot, slot + 4, pair_of, onward).start()
        elif piece == 5 + pair_of:
            ring_copy(stream, slot, 14, pair_of, onward).start()
        hand_over(stream, slot, pair_of).start()

    def open_queries(stream):
        await_bytes(
            landed.at[stream, pl.ds(0, 2), pl.ds(9, 63)], spread_recv.at[stream, QUERY]
        )
        query_hat = landed.at[stream, 0].reshape(BLOCK, HD)[...]
        query_dot = landed.at[stream, 1].reshape(BLOCK, HD)[...]
        queries[stream, :, 0:HD] = query_dot
        queries[stream, :, HD : 2 * HD] = query_hat
        peak[stream] = jnp.full((BLOCK, 1), -jnp.inf, jnp.float32)
        total[stream] = jnp.zeros((BLOCK, 1), jnp.float32)
        drift[stream] = jnp.zeros((BLOCK, 1), jnp.float32)
        summed[stream] = jnp.zeros((BLOCK, 2 * HD), jnp.float32)

    def absorb(stream, first_piece, count):
        for piece in range(first_piece, first_piece + count):
            await_bytes(
                store.at[stream, :, rows_at(2 * piece + 1)],
                partner_recv.at[stream, piece],
            )
        rows = pl.ds(first_piece * (2 * BLOCK), count * (2 * BLOCK))
        query_pair = queries[stream]
        query_hat = query_pair[:, HD:]
        key = store[stream, 0, rows]
        key_pair = jnp.concatenate([key, store[stream, 1, rows]], axis=1)
        value = store[stream, 2, rows]
        value_pair = jnp.concatenate([value, store[stream, 3, rows]], axis=1)
        contract = (((1,), (1,)), ((), ()))
        scores = (
            lax.dot_general(query_hat, key, contract, preferred_element_type=jnp.float32)
            * SCALE
        )
        scores_dot = (
            lax.dot_general(
                query_pair, key_pair, contract, preferred_element_type=jnp.float32
            )
            * SCALE
        )
        old_peak = peak[stream]
        new_peak = jnp.maximum(old_peak, jnp.max(scores, axis=1, keepdims=True))
        rescale = jnp.exp(old_peak - new_peak)
        weights = jnp.exp(scores - new_peak)
        product = weights * scores_dot
        peak[stream] = new_peak
        total[stream] = total[stream] * rescale + jnp.sum(weights, axis=1, keepdims=True)
        drift[stream] = drift[stream] * rescale + jnp.sum(product, axis=1, keepdims=True)
        low_weights = weights.astype(jnp.bfloat16)
        low_product = product.astype(jnp.bfloat16)
        first = jnp.dot(low_weights, value_pair, preferred_element_type=jnp.float32)
        second = jnp.dot(low_product, value, preferred_element_type=jnp.float32)
        summed[stream, :, 0:HD] = summed[stream, :, 0:HD] * rescale + first[:, 0:HD]
        summed[stream, :, HD:] = (
            summed[stream, :, HD:] * rescale + first[:, HD:] + second
        )

    def back_copy(stream, k):
        return pltpu.make_async_remote_copy(
            src_ref=result.at[stream, :, pl.ds(k * 9, 9)],
            dst_ref=returned.at[k, stream],
            send_sem=back_send,
            recv_sem=back_recv.at[stream],
            device_id=spread(stream, RING - k),
            device_id_type=MESH,
        )

    def finish(stream):
        inverse = 1.0 / total[stream]
        base = summed[stream, :, 0:HD]
        attended = base * inverse
        tangent = (summed[stream, :, HD:] - drift[stream] * inverse * base) * inverse
        result.at[stream, 0].reshape(BLOCK, HD)[...] = attended.astype(jnp.bfloat16)
        result.at[stream, 1].reshape(BLOCK, HD)[...] = tangent.astype(jnp.bfloat16)

        def one(k, carry):
            back_copy(stream, k).start()
            return carry

        lax.fori_loop(1, RING, one, 0)
        returned[0, stream] = result[stream, :, 0:9]

    for kind, stream, piece, detail in ORDER:
        if kind == PASS and piece == 0:
            begin(stream, detail)
        elif kind == PASS:
            pass_on(stream, piece, detail)
        else:
            if piece == 0:
                open_queries(stream)
            absorb(stream, piece, detail)
            if piece == PIECES - 1:
                finish(stream)

    for stream in range(STREAMS):
        await_bytes(returned.at[pl.ds(1, 7), stream], back_recv.at[stream])

        def unpack(k, carry):
            cols = columns_at(head_of(stream, k))
            for a, ref in enumerate((out_ref, out_tan_ref)):
                ref[0, 0:16, cols] = returned[k, stream, a, 0:8].reshape(16, HD)
                ref[0, 16:18, cols] = returned[k, stream, a, 8]
            return carry

        lax.fori_loop(0, RING, unpack, 0, unroll=4)

    await_bytes(packed.at[pl.ds(1, 7)], spread_send)
    await_bytes(result.at[:, :, pl.ds(9, 63)], back_send)
    for stream in range(STREAMS):
        await_bytes(
            store.at[stream, :, pl.ds(BLOCK, (2 * PIECES - 1) * BLOCK)],
            ring_send.at[stream],
        )


def local(*operands):
    operands = operands[:6] + tuple(g.reshape(1, HD) for g in operands[6:])
    shape = jax.ShapeDtypeStruct(operands[0].shape, jnp.bfloat16)
    vmem = pl.BlockSpec(memory_space=pltpu.VMEM)
    dma = pltpu.SemaphoreType.DMA
    bf16, f32 = jnp.bfloat16, jnp.float32
    out = pl.pallas_call(
        kernel,
        out_shape=(shape, shape),
        in_specs=[pl.BlockSpec(memory_space=pltpu.HBM)] * 8,
        out_specs=(vmem, vmem),
        scratch_shapes=[
            pltpu.VMEM((6, PART, operands[0].shape[2]), bf16),
            pltpu.VMEM((2, 1, HD), f32),
            pltpu.VMEM((RING, STREAMS, 6, 9, 2, HD), bf16),
            pltpu.VMEM((STREAMS, 6, 72, 2, HD), bf16),
            pltpu.VMEM((STREAMS, BLOCK, 2 * HD), bf16),
            pltpu.VMEM((STREAMS, 4, 2 * PIECES * BLOCK, HD), bf16),
            pltpu.VMEM((STREAMS, BLOCK, 1), f32),
            pltpu.VMEM((STREAMS, BLOCK, 1), f32),
            pltpu.VMEM((STREAMS, BLOCK, 1), f32),
            pltpu.VMEM((STREAMS, BLOCK, 2 * HD), f32),
            pltpu.VMEM((STREAMS, 2, 72, 2, HD), bf16),
            pltpu.VMEM((RING, STREAMS, 2, 9, 2, HD), bf16),
            dma((8,)),
            dma,
            dma((STREAMS, 3)),
            dma((STREAMS,)),
            dma((STREAMS, PIECES, 2)),
            dma((STREAMS, PIECES)),
            dma,
            dma((STREAMS,)),
        ],
        compiler_params=pltpu.CompilerParams(
            collective_id=0,
            has_side_effects=True,
            vmem_limit_bytes=40 * 1024 * 1024,
        ),
    )(*(pltpu.with_memory_space_constraint(a, pltpu.HBM) for a in operands))
    return out[0], out[1]


def solution(mesh):
    rows = P("blk", "head", None)
    return jax.shard_map(
        local,
        mesh=mesh,
        in_specs=(rows,) * 6 + (P(), P()),
        out_specs=(rows, rows),
        check_vma=False,
    )
```

time: 69.6 us -> 56.8 us (0.82)
  Pallas kernels: 61.3 us -> 54.7 us
  local copies, waits for them, and re-layouts: 7.44 us -> 1.32 us
    pallas_call x1, Pallas kernels: 61.3 us -> 54.7 us  [local(): pl.pallas_call(kernel, out_shape=(shape, shape), in_specs=[pl.BlockSpec(m...]
    unnamed x18 -> x2, local copies, waits for them, and re-layouts: 7.44 us -> 1.32 us
where the time goes in v2:
time: 56.8 us; the launch traced here: 56.7 us
  Pallas kernels  54.7 us (96%)
  local copies, waits for them, and re-layouts  1.32 us (2%)
  between operations  0.64 us (1%)
    pallas_call x1, Pallas kernels, local(): pl.pallas_call(kernel, out_shape=(shape, shape), in_specs=[pl.BlockSpec(m...  54.7 us
    unnamed x2, local copies, waits for them, and re-layouts  1.32 us

profile of v2, /device:TPU:1, one launch (start us, length us, event | category | flops | bytes accessed | tf_op | source)
XLA Modules:
  0.0 56.7 jit_solution(4558868974756003400)
XLA Ops:
  0.6 54.7 %shard_map.95 = (bf16[1,18,3072]{2,1,0:T(8,128)(2,1)S(1)}, bf16[1,18,3072]{2,1,0:T(8,128)(2,1)S(1)}) custom-call(bf16[1,18,3072]{2,1,0:T(8,128)(2,1)} %query_hbm.1, bf16[1,18,3072]{2,1,0:T(8,128)(2,1)} %key_hbm.1, bf16[1,18,3072]{2,1,0:T(8,128)(2,1)} %value_hbm.1, bf16[1,18,3072]{2,1,0:T(8,128)(2,1)} %query_tan_hbm.1, bf16[1,18,3072]{2,1,0:T(8,128)(2,1)} %key_tan_hbm.1, ...), custom_call_target="tpu_custom_call" | custom-call | tf_op jit(solution)/shard_map/pallas_call | solution.py:384
  55.3 0.7 %copy.12 = bf16[1,18,3072]{2,1,0:T(8,128)(2,1)} copy(bf16[1,18,3072]{2,1,0:T(8,128)(2,1)S(1)} %get-tuple-element.4) | data formatting | bytes 221184
  56.0 0.7 %copy.13 = bf16[1,18,3072]{2,1,0:T(8,128)(2,1)} copy(bf16[1,18,3072]{2,1,0:T(8,128)(2,1)S(1)} %get-tuple-element.5) | data formatting | bytes 221184

commit v3 on v2

--- a/solution.py
+++ b/solution.py
@@ -18,20 +18,21 @@
 PIECES = 8
 PASS, ABSORB = 0, 1
 ORDER = (
-    (PASS, 1, 0, 1), (PASS, 0, 0, 1), (PASS, 1, 0, 0), (PASS, 0, 0, 0), (ABSORB, 1, 0, 1),
-    (PASS, 0, 1, 1), (PASS, 0, 2, 1), (PASS, 2, 0, 1), (PASS, 0, 1, 0), (PASS, 0, 2, 0),
-    (PASS, 2, 0, 0), (PASS, 0, 3, 1), (PASS, 0, 4, 1), (ABSORB, 0, 0, 1), (PASS, 2, 1, 1),
-    (PASS, 2, 2, 1), (ABSORB, 0, 1, 2), (ABSORB, 2, 0, 1), (PASS, 0, 3, 0), (PASS, 0, 4, 0),
-    (PASS, 1, 1, 1), (PASS, 1, 2, 1), (PASS, 2, 1, 0), (PASS, 2, 2, 0), (PASS, 1, 1, 0),
-    (PASS, 1, 2, 0), (ABSORB, 0, 3, 2), (PASS, 0, 5, 1), (PASS, 0, 6, 1), (ABSORB, 2, 1, 2),
-    (PASS, 1, 3, 1), (PASS, 1, 4, 1), (PASS, 2, 3, 1), (PASS, 2, 4, 1), (ABSORB, 1, 1, 2),
-    (PASS, 1, 3, 0), (PASS, 1, 4, 0), (PASS, 0, 5, 0), (PASS, 0, 6, 0), (PASS, 2, 3, 0),
-    (PASS, 2, 4, 0), (PASS, 1, 5, 1), (PASS, 1, 6, 1), (ABSORB, 1, 3, 2), (PASS, 2, 5, 1),
-    (PASS, 0, 7, 1), (PASS, 1, 5, 0), (PASS, 1, 6, 0), (ABSORB, 0, 5, 2), (PASS, 0, 7, 0),
-    (PASS, 2, 6, 1), (ABSORB, 2, 3, 2), (PASS, 1, 7, 1), (PASS, 2, 5, 0), (PASS, 2, 6, 0),
-    (ABSORB, 1, 5, 2), (PASS, 1, 7, 0), (ABSORB, 0, 7, 1), (PASS, 2, 7, 1), (ABSORB, 2, 5, 2),
-    (ABSORB, 1, 7, 1), (PASS, 2, 7, 0), (ABSORB, 2, 7, 1),
+    (PASS, 1, 0, 1), (PASS, 0, 0, 1), (PASS, 0, 0, 0), (PASS, 1, 0, 0), (PASS, 0, 2, 1),
+    (PASS, 0, 1, 1), (PASS, 2, 0, 1), (PASS, 2, 0, 0), (PASS, 0, 1, 0), (PASS, 0, 2, 0),
+    (PASS, 2, 1, 1), (PASS, 2, 2, 1), (PASS, 1, 2, 1), (ABSORB, 0, 0, 1), (PASS, 2, 2, 0),
+    (PASS, 2, 1, 0), (PASS, 1, 1, 0), (PASS, 0, 3, 1), (PASS, 1, 1, 1), (PASS, 1, 2, 0),
+    (PASS, 0, 3, 0), (ABSORB, 1, 0, 1), (PASS, 0, 4, 0), (PASS, 0, 4, 1), (PASS, 2, 4, 1),
+    (PASS, 1, 4, 1), (ABSORB, 2, 0, 1), (ABSORB, 2, 1, 2), (PASS, 1, 3, 0), (ABSORB, 0, 3, 2),
+    (PASS, 2, 3, 0), (PASS, 2, 3, 1), (PASS, 1, 4, 0), (PASS, 2, 4, 0), (ABSORB, 0, 1, 2),
+    (PASS, 1, 3, 1), (PASS, 1, 6, 1), (ABSORB, 2, 3, 2), (PASS, 0, 6, 0), (PASS, 0, 5, 1),
+    (PASS, 1, 5, 0), (PASS, 0, 5, 0), (PASS, 0, 6, 1), (ABSORB, 1, 1, 2), (PASS, 1, 6, 0),
+    (ABSORB, 1, 3, 2), (PASS, 2, 6, 1), (PASS, 1, 5, 1), (PASS, 2, 5, 0), (ABSORB, 0, 5, 2),
+    (PASS, 1, 7, 1), (PASS, 2, 6, 0), (PASS, 2, 5, 1), (ABSORB, 1, 5, 2), (PASS, 1, 7, 0),
+    (ABSORB, 2, 5, 2), (PASS, 0, 7, 0), (PASS, 0, 7, 1), (ABSORB, 1, 7, 1), (PASS, 2, 7, 1),
+    (PASS, 2, 7, 0), (ABSORB, 0, 7, 1), (ABSORB, 2, 7, 1),
 )
+TURN = (1, 0, 0)
 QUERY, KEY, VALUE = 0, 1, 2
 
 EPSILON = 1e-06
@@ -80,6 +81,45 @@
     back_send,
     back_recv,
 ):
+    head = lax.axis_index("head")
+    blk = lax.axis_index("blk")
+    core = head % 2
+    x = blk % IMAGES
+    y = (head // 2) * 2 + (blk // IMAGES) % 2
+    z = blk // (2 * IMAGES)
+
+    def device(yy, zz, cc):
+        return {"head": (yy // 2) * 2 + cc, "blk": (zz * 2 + yy % 2) * IMAGES + x}
+
+    def spread(stream, hops):
+        flip = stream % 2
+        return device((y + hops * (1 - flip)) % RING, (z + hops * flip) % RING, core)
+
+    def along(stream, hops):
+        flip = stream % 2
+        return device((y + hops * flip) % RING, (z + hops * (1 - flip)) % RING, core)
+
+    partner = device(y, z, 1 - core)
+
+    def head_of(stream, hops):
+        if stream == 1:
+            return 2 * RING + (z + hops) % RING
+        return 2 * ((y + hops) % RING) + stream // 2
+
+    barrier = pltpu.get_barrier_semaphore()
+
+    def peer(i):
+        return RING // 2 + (i + 1) // 2 * (1 - 2 * (i % 2))
+
+    def greet(i, carry):
+        k = peer(i)
+        pl.semaphore_signal(barrier, inc=1, device_id=spread(0, k), device_id_type=MESH)
+        pl.semaphore_signal(barrier, inc=1, device_id=spread(1, k), device_id_type=MESH)
+        return carry
+
+    lax.fori_loop(0, RING - 1, greet, 0)
+    pl.semaphore_signal(barrier, inc=1, device_id=partner, device_id_type=MESH)
+
     sources = (query_hbm, query_tan_hbm, key_hbm, key_tan_hbm, value_hbm, value_tan_hbm)
     loads = [
         pltpu.make_async_copy(source.at[0], inputs.at[a], input_sem.at[a])
@@ -89,41 +129,6 @@
         loads.append(pltpu.make_async_copy(source, gains.at[i], input_sem.at[6 + i]))
     for a in (4, 5, 2, 3, 7, 0, 1, 6):
         loads[a].start()
-
-    head = lax.axis_index("head")
-    blk = lax.axis_index("blk")
-    core = head % 2
-    x = blk % IMAGES
-    y = (head // 2) * 2 + (blk // IMAGES) % 2
-    z = blk // (2 * IMAGES)
-
-    def device(yy, zz, cc):
-        return {"head": (yy // 2) * 2 + cc, "blk": (zz * 2 + yy % 2) * IMAGES + x}
-
-    def spread(stream, hops):
-        flip = stream % 2
-        return device((y + hops * (1 - flip)) % RING, (z + hops * flip) % RING, core)
-
-    def along(stream, hops):
-        flip = stream % 2
-        return device((y + hops * flip) % RING, (z + hops * (1 - flip)) % RING, core)
-
-    partner = device(y, z, 1 - core)
-
-    def head_of(stream, hops):
-        if stream == 1:
-            return 2 * RING + (z + hops) % RING
-        return 2 * ((y + hops) % RING) + stream // 2
-
-    barrier = pltpu.get_barrier_semaphore()
-
-    def greet(k, carry):
-        pl.semaphore_signal(barrier, inc=1, device_id=spread(0, k), device_id_type=MESH)
-        pl.semaphore_signal(barrier, inc=1, device_id=spread(1, k), device_id_type=MESH)
-        return carry
-
-    lax.fori_loop(1, RING, greet, 0)
-    pl.semaphore_signal(barrier, inc=1, device_id=partner, device_id_type=MESH)
 
     place = blk // IMAGES
     token = place * BLOCK + head * PART + lax.broadcasted_iota(jnp.int32, (PART, HD), 0)
@@ -187,11 +192,11 @@
         )
 
     def send_out(stream, group):
-        def one(k, carry):
-            spread_copy(stream, group, k).start()
+        def one(i, carry):
+            spread_copy(stream, group, peer(i)).start()
             return carry
 
-        lax.fori_loop(1, RING, one, 0)
+        lax.fori_loop(0, RING - 1, one, 0)
 
     def await_bytes(ref, sem):
         pltpu.make_async_copy(ref, ref, sem).wait()
@@ -259,7 +264,7 @@
         onward = along(stream, 1 if piece % 2 else RING - 1)
         if piece <= 4:
             ring_copy(stream, slot, slot + 4, pair_of, onward).start()
-        elif piece == 5 + pair_of:
+        elif piece == 5 + (pair_of ^ TURN[stream]):
             ring_copy(stream, slot, 14, pair_of, onward).start()
         hand_over(stream, slot, pair_of).start()
 
@@ -335,11 +340,11 @@
         result.at[stream, 0].reshape(BLOCK, HD)[...] = attended.astype(jnp.bfloat16)
         result.at[stream, 1].reshape(BLOCK, HD)[...] = tangent.astype(jnp.bfloat16)
 
-        def one(k, carry):
-            back_copy(stream, k).start()
+        def one(i, carry):
+            back_copy(stream, peer(i)).start()
             return carry
 
-        lax.fori_loop(1, RING, one, 0)
+        lax.fori_loop(0, RING - 1, one, 0)
         returned[0, stream] = result[stream, :, 0:9]
 
     for kind, stream, piece, detail in ORDER:

time: 56.8 us -> 54.6 us (0.961)
  Pallas kernels: 54.7 us -> 52.5 us
    pallas_call x1, Pallas kernels: 54.7 us -> 52.5 us  [local(): pl.pallas_call(kernel, out_shape=(shape, shape), in_specs=[pl.BlockSpec(m...]
where the time goes in v3:
time: 54.6 us; the launch traced here: 54.5 us
  Pallas kernels  52.5 us (96%)
  local copies, waits for them, and re-layouts  1.32 us (2%)
  between operations  0.64 us (1%)
    pallas_call x1, Pallas kernels, local(): pl.pallas_call(kernel, out_shape=(shape, shape), in_specs=[pl.BlockSpec(m...  52.5 us
    unnamed x2, local copies, waits for them, and re-layouts  1.32 us

profile of v3, /device:TPU:1, one launch (start us, length us, event | category | flops | bytes accessed | tf_op | source)
XLA Modules:
  0.0 54.5 jit_solution(13276920665497554695)
XLA Ops:
  0.6 52.5 %shard_map.95 = (bf16[1,18,3072]{2,1,0:T(8,128)(2,1)S(1)}, bf16[1,18,3072]{2,1,0:T(8,128)(2,1)S(1)}) custom-call(bf16[1,18,3072]{2,1,0:T(8,128)(2,1)} %query_hbm.1, bf16[1,18,3072]{2,1,0:T(8,128)(2,1)} %key_hbm.1, bf16[1,18,3072]{2,1,0:T(8,128)(2,1)} %value_hbm.1, bf16[1,18,3072]{2,1,0:T(8,128)(2,1)} %query_tan_hbm.1, bf16[1,18,3072]{2,1,0:T(8,128)(2,1)} %key_tan_hbm.1, ...), custom_call_target="tpu_custom_call" | custom-call | tf_op jit(solution)/shard_map/pallas_call | solution.py:389
  53.2 0.7 %copy.12 = bf16[1,18,3072]{2,1,0:T(8,128)(2,1)} copy(bf16[1,18,3072]{2,1,0:T(8,128)(2,1)S(1)} %get-tuple-element.4) | data formatting | bytes 221184
  53.8 0.7 %copy.13 = bf16[1,18,3072]{2,1,0:T(8,128)(2,1)} copy(bf16[1,18,3072]{2,1,0:T(8,128)(2,1)S(1)} %get-tuple-element.5) | data formatting | bytes 221184

commit v4 on v3

--- a/solution.py
+++ b/solution.py
@@ -18,21 +18,22 @@
 PIECES = 8
 PASS, ABSORB = 0, 1
 ORDER = (
-    (PASS, 1, 0, 1), (PASS, 0, 0, 1), (PASS, 0, 0, 0), (PASS, 1, 0, 0), (PASS, 0, 2, 1),
-    (PASS, 0, 1, 1), (PASS, 2, 0, 1), (PASS, 2, 0, 0), (PASS, 0, 1, 0), (PASS, 0, 2, 0),
-    (PASS, 2, 1, 1), (PASS, 2, 2, 1), (PASS, 1, 2, 1), (ABSORB, 0, 0, 1), (PASS, 2, 2, 0),
-    (PASS, 2, 1, 0), (PASS, 1, 1, 0), (PASS, 0, 3, 1), (PASS, 1, 1, 1), (PASS, 1, 2, 0),
-    (PASS, 0, 3, 0), (ABSORB, 1, 0, 1), (PASS, 0, 4, 0), (PASS, 0, 4, 1), (PASS, 2, 4, 1),
-    (PASS, 1, 4, 1), (ABSORB, 2, 0, 1), (ABSORB, 2, 1, 2), (PASS, 1, 3, 0), (ABSORB, 0, 3, 2),
-    (PASS, 2, 3, 0), (PASS, 2, 3, 1), (PASS, 1, 4, 0), (PASS, 2, 4, 0), (ABSORB, 0, 1, 2),
-    (PASS, 1, 3, 1), (PASS, 1, 6, 1), (ABSORB, 2, 3, 2), (PASS, 0, 6, 0), (PASS, 0, 5, 1),
-    (PASS, 1, 5, 0), (PASS, 0, 5, 0), (PASS, 0, 6, 1), (ABSORB, 1, 1, 2), (PASS, 1, 6, 0),
-    (ABSORB, 1, 3, 2), (PASS, 2, 6, 1), (PASS, 1, 5, 1), (PASS, 2, 5, 0), (ABSORB, 0, 5, 2),
-    (PASS, 1, 7, 1), (PASS, 2, 6, 0), (PASS, 2, 5, 1), (ABSORB, 1, 5, 2), (PASS, 1, 7, 0),
-    (ABSORB, 2, 5, 2), (PASS, 0, 7, 0), (PASS, 0, 7, 1), (ABSORB, 1, 7, 1), (PASS, 2, 7, 1),
+    (PASS, 1, 0, 1), (PASS, 0, 0, 1), (PASS, 0, 0, 0), (PASS, 1, 0, 0), (PASS, 2, 0, 1),
+    (ABSORB, 1, 0, 1), (PASS, 2, 0, 0), (PASS, 0, 1, 1), (PASS, 0, 2, 1), (PASS, 0, 1, 0),
+    (PASS, 0, 2, 0), (ABSORB, 0, 0, 1), (PASS, 2, 2, 1), (ABSORB, 0, 1, 2), (PASS, 2, 1, 1),
+    (PASS, 1, 2, 1), (PASS, 1, 1, 1), (ABSORB, 2, 0, 1), (PASS, 2, 1, 0), (PASS, 2, 2, 0),
+    (PASS, 1, 2, 0), (PASS, 1, 1, 0), (PASS, 0, 4, 1), (PASS, 0, 3, 1), (ABSORB, 2, 1, 2),
+    (PASS, 0, 4, 0), (PASS, 0, 3, 0), (PASS, 1, 4, 1), (PASS, 1, 3, 1), (ABSORB, 1, 1, 2),
+    (PASS, 2, 3, 1), (PASS, 1, 4, 0), (PASS, 1, 3, 0), (ABSORB, 0, 3, 2), (PASS, 2, 4, 0),
+    (PASS, 2, 3, 0), (PASS, 2, 4, 1), (ABSORB, 1, 3, 2), (PASS, 0, 5, 1), (PASS, 1, 6, 1),
+    (PASS, 0, 6, 1), (PASS, 1, 5, 1), (ABSORB, 2, 3, 2), (PASS, 1, 6, 0), (PASS, 0, 5, 0),
+    (PASS, 1, 5, 0), (PASS, 0, 6, 0), (PASS, 2, 6, 0), (PASS, 2, 5, 1), (ABSORB, 1, 5, 2),
+    (PASS, 2, 6, 1), (PASS, 2, 5, 0), (PASS, 1, 7, 1), (ABSORB, 0, 5, 2), (PASS, 1, 7, 0),
+    (ABSORB, 2, 5, 2), (PASS, 0, 7, 1), (PASS, 0, 7, 0), (ABSORB, 1, 7, 1), (PASS, 2, 7, 1),
     (PASS, 2, 7, 0), (ABSORB, 0, 7, 1), (ABSORB, 2, 7, 1),
 )
-TURN = (1, 0, 0)
+NEAR = 80
+TURN = (0, 1, 1)
 QUERY, KEY, VALUE = 0, 1, 2
 
 EPSILON = 1e-06
@@ -180,11 +181,12 @@
         pair = pl.ds(2 * group, 2)
         landed[stream, pair, 0:9] = packed[0, stream, pair]
 
-    def spread_copy(stream, group, k):
+    def spread_copy(stream, group, i):
+        k = peer(i)
         pair = pl.ds(2 * group, 2)
         return pltpu.make_async_remote_copy(
             src_ref=packed.at[k, stream, pair],
-            dst_ref=landed.at[stream, pair, pl.ds(k * 9, 9)],
+            dst_ref=landed.at[stream, pair, pl.ds((RING - 1 - i) * 9, 9)],
             send_sem=spread_send,
             recv_sem=spread_recv.at[stream, group],
             device_id=spread(stream, k),
@@ -193,7 +195,7 @@
 
     def send_out(stream, group):
         def one(i, carry):
-            spread_copy(stream, group, peer(i)).start()
+            spread_copy(stream, group, i).start()
             return carry
 
         lax.fori_loop(0, RING - 1, one, 0)
@@ -244,11 +246,14 @@
             device_id_type=MESH,
         )
 
+    def await_spread(stream, group):
+        await_bytes(
+            landed.at[stream, pl.ds(2 * group, 2), pl.ds(9, 63)],
+            spread_recv.at[stream, group],
+        )
+
     def begin(stream, pair_of):
-        pair = pl.ds(2 * (pair_of + 1), 2)
-        await_bytes(
-            landed.at[stream, pair, pl.ds(9, 63)], spread_recv.at[stream, pair_of + 1]
-        )
+        await_spread(stream, pair_of + 1)
         for a in (2 * pair_of, 2 * pair_of + 1):
             store[stream, a, 0:BLOCK] = landed.at[stream, 2 + a].reshape(BLOCK, HD)[...]
         ring_copy(stream, 0, 2, pair_of, along(stream, 1)).start()
@@ -269,9 +274,7 @@
         hand_over(stream, slot, pair_of).start()
 
     def open_queries(stream):
-        await_bytes(
-            landed.at[stream, pl.ds(0, 2), pl.ds(9, 63)], spread_recv.at[stream, QUERY]
-        )
+        await_spread(stream, QUERY)
         query_hat = landed.at[stream, 0].reshape(BLOCK, HD)[...]
         query_dot = landed.at[stream, 1].reshape(BLOCK, HD)[...]
         queries[stream, :, 0:HD] = query_dot
@@ -322,9 +325,10 @@
             summed[stream, :, HD:] * rescale + first[:, HD:] + second
         )
 
-    def back_copy(stream, k):
+    def back_copy(stream, i):
+        k = peer(i)
         return pltpu.make_async_remote_copy(
-            src_ref=result.at[stream, :, pl.ds(k * 9, 9)],
+            src_ref=result.at[stream, :, pl.ds((RING - 1 - i) * 9, 9)],
             dst_ref=returned.at[k, stream],
             send_sem=back_send,
             recv_sem=back_recv.at[stream],
@@ -333,18 +337,19 @@
         )
 
     def finish(stream):
-        inverse = 1.0 / total[stream]
-        base = summed[stream, :, 0:HD]
-        attended = base * inverse
-        tangent = (summed[stream, :, HD:] - drift[stream] * inverse * base) * inverse
-        result.at[stream, 0].reshape(BLOCK, HD)[...] = attended.astype(jnp.bfloat16)
-        result.at[stream, 1].reshape(BLOCK, HD)[...] = tangent.astype(jnp.bfloat16)
-
         def one(i, carry):
-            back_copy(stream, peer(i)).start()
+            back_copy(stream, i).start()
             return carry
 
-        lax.fori_loop(0, RING - 1, one, 0)
+        for low, high, first, last in ((NEAR, BLOCK, 0, 3), (0, NEAR, 3, RING - 1)):
+            inverse = 1.0 / total[stream, low:high]
+            base = summed[stream, low:high, 0:HD]
+            ratio = drift[stream, low:high] * inverse
+            tangent = (summed[stream, low:high, HD:] - ratio * base) * inverse
+            for a, v in enumerate((base * inverse, tangent)):
+                rows = v.astype(jnp.bfloat16)
+                result.at[stream, a].reshape(BLOCK, HD)[low:high] = rows
+            lax.fori_loop(first, last, one, 0)
         returned[0, stream] = result[stream, :, 0:9]
 
     for kind, stream, piece, detail in ORDER:
@@ -378,6 +383,17 @@
             store.at[stream, :, pl.ds(BLOCK, (2 * PIECES - 1) * BLOCK)],
             ring_send.at[stream],
         )
+
+
+def write_out(first, second, out_first, out_second, sems):
+    copies = [
+        pltpu.make_async_copy(source, target, sems.at[i])
+        for i, (source, target) in enumerate(((first, out_first), (second, out_second)))
+    ]
+    for copy in copies:
+        copy.start()
+    for copy in copies:
+        copy.wait()
 
 
 def local(*operands):
@@ -419,7 +435,15 @@
             vmem_limit_bytes=40 * 1024 * 1024,
         ),
     )(*(pltpu.with_memory_space_constraint(a, pltpu.HBM) for a in operands))
-    return out[0], out[1]
+    hbm = pl.BlockSpec(memory_space=pltpu.HBM)
+    return pl.pallas_call(
+        write_out,
+        out_shape=(shape, shape),
+        in_specs=[vmem, vmem],
+        out_specs=(hbm, hbm),
+        scratch_shapes=[dma((2,))],
+        compiler_params=pltpu.CompilerParams(vmem_limit_bytes=1024 * 1024),
+    )(*(pltpu.with_memory_space_constraint(a, pltpu.VMEM) for a in out))
 
 
 def solution(mesh):

time: 54.6 us -> 53.5 us (0.980)
  local copies, waits for them, and re-layouts: 1.32 us -> 0 us
    unnamed x2 -> x0, local copies, waits for them, and re-layouts: 1.32 us -> none
    pallas_call x0 -> x1, Pallas kernels: none -> 0.73 us  [local(): pl.pallas_call(write_out, out_shape=(shape, shape), in_specs=[vmem, vmem]...]
where the time goes in v4:
time: 53.5 us; the launch traced here: 53.3 us
  Pallas kernels  52.7 us (99%)
  between operations  0.64 us (1%)
    pallas_call x1, Pallas kernels, local(): pl.pallas_call(kernel, out_shape=(shape, shape), in_specs=[pl.BlockSpec(m...  52 us

profile of v4, /device:TPU:1, one launch (start us, length us, event | category | flops | bytes accessed | tf_op | source)
XLA Modules:
  0.0 53.3 jit_solution(2448182968680708380)
XLA Ops:
  0.6 52.0 %shard_map.95 = (bf16[1,18,3072]{2,1,0:T(8,128)(2,1)S(1)}, bf16[1,18,3072]{2,1,0:T(8,128)(2,1)S(1)}) custom-call(bf16[1,18,3072]{2,1,0:T(8,128)(2,1)} %query_hbm.1, bf16[1,18,3072]{2,1,0:T(8,128)(2,1)} %key_hbm.1, bf16[1,18,3072]{2,1,0:T(8,128)(2,1)} %value_hbm.1, bf16[1,18,3072]{2,1,0:T(8,128)(2,1)} %query_tan_hbm.1, bf16[1,18,3072]{2,1,0:T(8,128)(2,1)} %key_tan_hbm.1, ...), custom_call_target="tpu_custom_call" | custom-call | tf_op jit(solution)/shard_map/pallas_call | solution.py:405
  52.6 0.7 %shard_map.96 = (bf16[1,18,3072]{2,1,0:T(8,128)(2,1)}, bf16[1,18,3072]{2,1,0:T(8,128)(2,1)}) custom-call(bf16[1,18,3072]{2,1,0:T(8,128)(2,1)S(1)} %get-tuple-element.4.first, bf16[1,18,3072]{2,1,0:T(8,128)(2,1)S(1)} %get-tuple-element.5.second), custom_call_target="tpu_custom_call" | custom-call | tf_op jit(solution)/shard_map/pallas_call | solution.py:439

commit v5 on v4

--- a/solution.py
+++ b/solution.py
@@ -29,9 +29,10 @@
     (PASS, 0, 6, 1), (PASS, 1, 5, 1), (ABSORB, 2, 3, 2), (PASS, 1, 6, 0), (PASS, 0, 5, 0),
     (PASS, 1, 5, 0), (PASS, 0, 6, 0), (PASS, 2, 6, 0), (PASS, 2, 5, 1), (ABSORB, 1, 5, 2),
     (PASS, 2, 6, 1), (PASS, 2, 5, 0), (PASS, 1, 7, 1), (ABSORB, 0, 5, 2), (PASS, 1, 7, 0),
-    (ABSORB, 2, 5, 2), (PASS, 0, 7, 1), (PASS, 0, 7, 0), (ABSORB, 1, 7, 1), (PASS, 2, 7, 1),
-    (PASS, 2, 7, 0), (ABSORB, 0, 7, 1), (ABSORB, 2, 7, 1),
+    (PASS, 0, 7, 1), (PASS, 0, 7, 0), (ABSORB, 2, 5, 2), (PASS, 2, 7, 1), (PASS, 2, 7, 0),
+    (ABSORB, 0, 7, 1), (ABSORB, 1, 7, 1), (ABSORB, 2, 7, 1),
 )
+OWN = 16
 NEAR = 80
 TURN = (0, 1, 1)
 QUERY, KEY, VALUE = 0, 1, 2
@@ -203,6 +204,26 @@
     def await_bytes(ref, sem):
         pltpu.make_async_copy(ref, ref, sem).wait()
 
+    def ring_copy(stream, source, target, pair_of, to, low=0, high=BLOCK):
+        pair = pl.ds(2 * pair_of, 2)
+        return pltpu.make_async_remote_copy(
+            src_ref=store.at[stream, pair, pl.ds(source * BLOCK + low, high - low)],
+            dst_ref=store.at[stream, pair, pl.ds(target * BLOCK + low, high - low)],
+            send_sem=ring_send.at[stream],
+            recv_sem=ring_recv.at[stream, target // 2, pair_of],
+            device_id=to,
+            device_id_type=MESH,
+        )
+
+    def move_own(stream, pair_of, low, high):
+        for a in (2 * pair_of, 2 * pair_of + 1):
+            rows = landed.at[stream, 2 + a].reshape(BLOCK, HD)[low:high]
+            store[stream, a, low:high] = rows
+
+    def send_own(stream, pair_of, low, high):
+        ring_copy(stream, 0, 2, pair_of, along(stream, 1), low, high).start()
+        ring_copy(stream, 0, 4, pair_of, along(stream, RING - 1), low, high).start()
+
     for a in (4, 5):
         loads[a].wait()
     for stream in range(STREAMS):
@@ -211,29 +232,24 @@
         loads[a].wait()
     for stream in (0, 1):
         pack(stream, KEY)
+    for stream, pair_of in ((0, 1), (2, 1), (0, 0)):
+        move_own(stream, pair_of, 0, OWN)
     pl.semaphore_wait(barrier, 2 * RING - 1)
     for group in (VALUE, KEY):
         for stream in (0, 1):
             send_out(stream, group)
     send_out(2, VALUE)
+    for stream, pair_of in ((0, 1), (2, 1), (0, 0)):
+        send_own(stream, pair_of, 0, OWN)
     pack(2, KEY)
+    move_own(2, 0, 0, OWN)
     send_out(2, KEY)
+    send_own(2, 0, 0, OWN)
     for a in (0, 1, 6):
         loads[a].wait()
     for stream in (1, 0, 2):
         pack(stream, QUERY)
         send_out(stream, QUERY)
-
-    def ring_copy(stream, source, target, pair_of, to):
-        pair = pl.ds(2 * pair_of, 2)
-        return pltpu.make_async_remote_copy(
-            src_ref=store.at[stream, pair, rows_at(source)],
-            dst_ref=store.at[stream, pair, rows_at(target)],
-            send_sem=ring_send.at[stream],
-            recv_sem=ring_recv.at[stream, target // 2, pair_of],
-            device_id=to,
-            device_id_type=MESH,
-        )
 
     def hand_over(stream, source, pair_of):
         pair = pl.ds(2 * pair_of, 2)
@@ -254,10 +270,9 @@
 
     def begin(stream, pair_of):
         await_spread(stream, pair_of + 1)
-        for a in (2 * pair_of, 2 * pair_of + 1):
-            store[stream, a, 0:BLOCK] = landed.at[stream, 2 + a].reshape(BLOCK, HD)[...]
-        ring_copy(stream, 0, 2, pair_of, along(stream, 1)).start()
-        ring_copy(stream, 0, 4, pair_of, along(stream, RING - 1)).start()
+        low = 0 if stream == 1 else OWN
+        move_own(stream, pair_of, low, BLOCK)
+        send_own(stream, pair_of, low, BLOCK)
         hand_over(stream, 0, pair_of).start()
 
     def pass_on(stream, piece, pair_of):
@@ -284,30 +299,21 @@
         drift[stream] = jnp.zeros((BLOCK, 1), jnp.float32)
         summed[stream] = jnp.zeros((BLOCK, 2 * HD), jnp.float32)
 
-    def absorb(stream, first_piece, count):
-        for piece in range(first_piece, first_piece + count):
-            await_bytes(
-                store.at[stream, :, rows_at(2 * piece + 1)],
-                partner_recv.at[stream, piece],
-            )
+    def score(stream, first_piece, count):
         rows = pl.ds(first_piece * (2 * BLOCK), count * (2 * BLOCK))
         query_pair = queries[stream]
-        query_hat = query_pair[:, HD:]
         key = store[stream, 0, rows]
         key_pair = jnp.concatenate([key, store[stream, 1, rows]], axis=1)
-        value = store[stream, 2, rows]
-        value_pair = jnp.concatenate([value, store[stream, 3, rows]], axis=1)
         contract = (((1,), (1,)), ((), ()))
-        scores = (
-            lax.dot_general(query_hat, key, contract, preferred_element_type=jnp.float32)
-            * SCALE
-        )
-        scores_dot = (
-            lax.dot_general(
-                query_pair, key_pair, contract, preferred_element_type=jnp.float32
-            )
-            * SCALE
-        )
+        scores = lax.dot_general(
+            query_pair[:, HD:], key, contract, preferred_element_type=jnp.float32
+        )
+        scores_dot = lax.dot_general(
+            query_pair, key_pair, contract, preferred_element_type=jnp.float32
+        )
+        return scores * SCALE, scores_dot * SCALE
+
+    def weigh(stream, scores, scores_dot):
         old_peak = peak[stream]
         new_peak = jnp.maximum(old_peak, jnp.max(scores, axis=1, keepdims=True))
         rescale = jnp.exp(old_peak - new_peak)
@@ -316,14 +322,30 @@
         peak[stream] = new_peak
         total[stream] = total[stream] * rescale + jnp.sum(weights, axis=1, keepdims=True)
         drift[stream] = drift[stream] * rescale + jnp.sum(product, axis=1, keepdims=True)
-        low_weights = weights.astype(jnp.bfloat16)
-        low_product = product.astype(jnp.bfloat16)
+        return rescale, weights.astype(jnp.bfloat16), product.astype(jnp.bfloat16)
+
+    def gather_values(stream, first_piece, count, rescale, low_weights, low_product):
+        rows = pl.ds(first_piece * (2 * BLOCK), count * (2 * BLOCK))
+        value = store[stream, 2, rows]
+        value_pair = jnp.concatenate([value, store[stream, 3, rows]], axis=1)
         first = jnp.dot(low_weights, value_pair, preferred_element_type=jnp.float32)
         second = jnp.dot(low_product, value, preferred_element_type=jnp.float32)
         summed[stream, :, 0:HD] = summed[stream, :, 0:HD] * rescale + first[:, 0:HD]
         summed[stream, :, HD:] = (
             summed[stream, :, HD:] * rescale + first[:, HD:] + second
         )
+
+    def absorb(units):
+        for stream, first_piece, count in units:
+            for piece in range(first_piece, first_piece + count):
+                await_bytes(
+                    store.at[stream, :, rows_at(2 * piece + 1)],
+                    partner_recv.at[stream, piece],
+                )
+        scored = [score(*unit) for unit in units]
+        weighed = [weigh(unit[0], *pair) for unit, pair in zip(units, scored)]
+        for unit, parts in zip(units, weighed):
+            gather_values(*unit, *parts)
 
     def back_copy(stream, i):
         k = peer(i)
@@ -337,10 +359,6 @@
         )
 
     def finish(stream):
-        def one(i, carry):
-            back_copy(stream, i).start()
-            return carry
-
         for low, high, first, last in ((NEAR, BLOCK, 0, 3), (0, NEAR, 3, RING - 1)):
             inverse = 1.0 / total[stream, low:high]
             base = summed[stream, low:high, 0:HD]
@@ -349,20 +367,24 @@
             for a, v in enumerate((base * inverse, tangent)):
                 rows = v.astype(jnp.bfloat16)
                 result.at[stream, a].reshape(BLOCK, HD)[low:high] = rows
-            lax.fori_loop(first, last, one, 0)
+            for i in range(first, last):
+                back_copy(stream, i).start()
         returned[0, stream] = result[stream, :, 0:9]
 
-    for kind, stream, piece, detail in ORDER:
-        if kind == PASS and piece == 0:
-            begin(stream, detail)
+    for kind, *detail in ORDER:
+        if kind == PASS and detail[1] == 0:
+            begin(detail[0], detail[2])
         elif kind == PASS:
-            pass_on(stream, piece, detail)
+            pass_on(*detail)
         else:
-            if piece == 0:
-                open_queries(stream)
-            absorb(stream, piece, detail)
-            if piece == PIECES - 1:
-                finish(stream)
+            units = [tuple(detail[i : i + 3]) for i in range(0, len(detail), 3)]
+            for stream, piece, _ in units:
+                if piece == 0:
+                    open_queries(stream)
+            absorb(units)
+            for stream, piece, _ in units:
+                if piece == PIECES - 1:
+                    finish(stream)
 
     for stream in range(STREAMS):
         await_bytes(returned.at[pl.ds(1, 7), stream], back_recv.at[stream])

time: 53.5 us -> 53.2 us (level)
  no operation moved by 1% of the time
where the time goes in v5:
time: 53.2 us; the launch traced here: 53 us
  Pallas kernels  52.4 us (98%)
  between operations  0.64 us (1%)
    pallas_call x1, Pallas kernels, local(): pl.pallas_call(kernel, out_shape=(shape, shape), in_specs=[pl.BlockSpec(m...  51.7 us

profile of v5, /device:TPU:1, one launch (start us, length us, event | category | flops | bytes accessed | tf_op | source)
XLA Modules:
  0.0 53.0 jit_solution(3316893328211272861)
XLA Ops:
  0.6 51.7 %shard_map.95 = (bf16[1,18,3072]{2,1,0:T(8,128)(2,1)S(1)}, bf16[1,18,3072]{2,1,0:T(8,128)(2,1)S(1)}) custom-call(bf16[1,18,3072]{2,1,0:T(8,128)(2,1)} %query_hbm.1, bf16[1,18,3072]{2,1,0:T(8,128)(2,1)} %key_hbm.1, bf16[1,18,3072]{2,1,0:T(8,128)(2,1)} %value_hbm.1, bf16[1,18,3072]{2,1,0:T(8,128)(2,1)} %query_tan_hbm.1, bf16[1,18,3072]{2,1,0:T(8,128)(2,1)} %key_tan_hbm.1, ...), custom_call_target="tpu_custom_call" | custom-call | tf_op jit(solution)/shard_map/pallas_call | solution.py:427
  52.3 0.7 %shard_map.96 = (bf16[1,18,3072]{2,1,0:T(8,128)(2,1)}, bf16[1,18,3072]{2,1,0:T(8,128)(2,1)}) custom-call(bf16[1,18,3072]{2,1,0:T(8,128)(2,1)S(1)} %get-tuple-element.4.first, bf16[1,18,3072]{2,1,0:T(8,128)(2,1)S(1)} %get-tuple-element.5.second), custom_call_target="tpu_custom_call" | custom-call | tf_op jit(solution)/shard_map/pallas_call | solution.py:461

commit v6 on v5

--- a/solution.py
+++ b/solution.py
@@ -19,7 +19,7 @@
 PASS, ABSORB = 0, 1
 ORDER = (
     (PASS, 1, 0, 1), (PASS, 0, 0, 1), (PASS, 0, 0, 0), (PASS, 1, 0, 0), (PASS, 2, 0, 1),
-    (ABSORB, 1, 0, 1), (PASS, 2, 0, 0), (PASS, 0, 1, 1), (PASS, 0, 2, 1), (PASS, 0, 1, 0),
+    (PASS, 0, 1, 1), (PASS, 0, 2, 1), (ABSORB, 1, 0, 1), (PASS, 2, 0, 0), (PASS, 0, 1, 0),
     (PASS, 0, 2, 0), (ABSORB, 0, 0, 1), (PASS, 2, 2, 1), (ABSORB, 0, 1, 2), (PASS, 2, 1, 1),
     (PASS, 1, 2, 1), (PASS, 1, 1, 1), (ABSORB, 2, 0, 1), (PASS, 2, 1, 0), (PASS, 2, 2, 0),
     (PASS, 1, 2, 0), (PASS, 1, 1, 0), (PASS, 0, 4, 1), (PASS, 0, 3, 1), (ABSORB, 2, 1, 2),

time: 53.2 us -> 52.7 us (level)
  no operation moved by 1% of the time
where the time goes in v6:
time: 52.7 us; the launch traced here: 52.5 us
  Pallas kernels  51.9 us (98%)
  between operations  0.64 us (1%)
    pallas_call x1, Pallas kernels, local(): pl.pallas_call(kernel, out_shape=(shape, shape), in_specs=[pl.BlockSpec(m...  51.2 us

profile of v6, /device:TPU:1, one launch (start us, length us, event | category | flops | bytes accessed | tf_op | source)
XLA Modules:
  0.0 52.5 jit_solution(8461309369069230926)
XLA Ops:
  0.6 51.2 %shard_map.95 = (bf16[1,18,3072]{2,1,0:T(8,128)(2,1)S(1)}, bf16[1,18,3072]{2,1,0:T(8,128)(2,1)S(1)}) custom-call(bf16[1,18,3072]{2,1,0:T(8,128)(2,1)} %query_hbm.1, bf16[1,18,3072]{2,1,0:T(8,128)(2,1)} %key_hbm.1, bf16[1,18,3072]{2,1,0:T(8,128)(2,1)} %value_hbm.1, bf16[1,18,3072]{2,1,0:T(8,128)(2,1)} %query_tan_hbm.1, bf16[1,18,3072]{2,1,0:T(8,128)(2,1)} %key_tan_hbm.1, ...), custom_call_target="tpu_custom_call" | custom-call | tf_op jit(solution)/shard_map/pallas_call | solution.py:427
  51.8 0.7 %shard_map.96 = (bf16[1,18,3072]{2,1,0:T(8,128)(2,1)}, bf16[1,18,3072]{2,1,0:T(8,128)(2,1)}) custom-call(bf16[1,18,3072]{2,1,0:T(8,128)(2,1)S(1)} %get-tuple-element.4.first, bf16[1,18,3072]{2,1,0:T(8,128)(2,1)S(1)} %get-tuple-element.5.second), custom_call_target="tpu_custom_call" | custom-call | tf_op jit(solution)/shard_map/pallas_call | solution.py:461
